TPU v7x, 8 devices: a whole 2x2x1 slice. The times are simulated.
8 devices in a mesh: rep: 2 (over y, z), dp: 4 (over x, core).
Axes of the slice: x: 2, y: 2, z: 1, core: 2. Of those that a mesh axis runs over, the one named last changes fastest.
Arguments:
- a: bfloat16 [8, 4, 4096, 1536], P(('rep', 'dp')), parts along dimension 0
- g: bfloat16 [8, 4, 4096, 3584], P(('rep', 'dp')), parts along dimension 0
Outputs:
- output: bfloat16 [8, 1536, 3584], P('rep'), parts along dimension 0
There are 2 independent parts. A program takes and returns all parts, laid end to end along the dimension named above; each array names one.
All inputs are finite; a program needn't handle non-finite values.
Results may differ from a plain program's by a relative error of at most 0.012.
Values are sent between devices in bfloat16 or wider.
A program may use at most 2 GiB of HBM per device.

v0:
```python
import jax
import jax.numpy as jnp


def solution(mesh):
    groups = mesh.shape["rep"]

    def step(a, g):
        a, g = (t.reshape(groups, -1, *t.shape[1:]) for t in (a, g))
        sums = jnp.einsum("rsntd,rsntf->rndf", a, g, preferred_element_type=jnp.float32)
        return sums.astype(jnp.bfloat16).reshape(-1, *sums.shape[2:])

    return step
```

profile of v0, /device:TPU:0, one launch (start us, length us, event | category | flops | bytes accessed | tf_op | source)
XLA Modules:
  0.0 1676.7 jit_solution(4878008831505191013)
XLA Ops:
  0.0 198.6 %fusion.2 = f32[1,4,1536,3584]{3,2,1,0:T(8,128)} fusion(bf16[1,4,4096,3584]{3,2,1,0:T(8,128)(2,1)} %param.1, bf16[1,4,4096,1536]{3,2,1,0:T(8,128)(2,1)} %param), kind=kOutput, calls=%fused_computation.2 | convolution fusion | flops 180388626432 | bytes 255852544 | tf_op jit(solution)/rsntd,rsntf->rndf/dot_general | solution.py:10
  198.6 1478.1 %all-reduce.2 = bf16[1,4,1536,3584]{3,2,1,0:T(8,128)(2,1)} all-reduce(f32[1,4,1536,3584]{3,2,1,0:T(8,128)} %fusion.2), channel_id=1, replica_groups=[2,4]<=[8], use_global_device_ids=true, to_apply=%add.clone | all-reduce | flops 22020096 | bytes 132120576 | tf_op jit(solution)/rsntd,rsntf->rndf/dot_general | solution.py:10
where the time goes:
time: 1680 us
  blocking collectives  1480 us (88%)
  matrix products  199 us (12%)
    dot_general x1, blocking collectives, step(): jnp.einsum('rsntd,rsntf->rndf', a, g, preferred_element_type=jnp.float32)  1480 us
    dot_general x1, matrix products, step(): jnp.einsum('rsntd,rsntf->rndf', a, g, preferred_element_type=jnp.float32)  199 us

commit v1 on v0

v1 whole, which is shorter than its diff:
```python
import jax
import jax.numpy as jnp
from jax import lax
from jax.experimental import pallas as pl
from jax.experimental.pallas import tpu as pltpu
from jax.sharding import PartitionSpec as P


WIDTHS = (
    (256, 256, 512, 1024, 1536),
    (2048, 1536),
    (2048, 1536),
    (1536, 1024, 512, 256, 256),
)
F_LAG = 3
VMEM = 67043328
ANY = pl.BlockSpec(memory_space=pl.ANY)


def _dot(a, g):
    return lax.dot_general(a, g, (((0,), (0,)), ((), ())), preferred_element_type=jnp.float32)


def _params(**kw):
    return dict(compiler_params=pltpu.CompilerParams(vmem_limit_bytes=VMEM), **kw)


def theirs(pos, a, g, dep, n, c0, c):
    k, d = a.shape[2:]
    half, ct = d // 2, min(c, 512)

    def body(pos, a_ref, g_ref, dep_ref, o_ref):
        o_ref[...] = _dot(a_ref[0, 0], g_ref[0, 0]).astype(o_ref.dtype)

    return pl.pallas_call(
        body,
        out_shape=jax.ShapeDtypeStruct((half, c), jnp.bfloat16),
        grid_spec=pltpu.PrefetchScalarGridSpec(
            num_scalar_prefetch=1,
            grid=(c // ct,),
            in_specs=[
                pl.BlockSpec((1, 1, k, half), lambda j, pos: (0, n, 0, 1 - pos[0])),
                pl.BlockSpec((1, 1, k, ct), lambda j, pos: (0, n, 0, c0 // ct + j)),
                ANY,
            ],
            out_specs=pl.BlockSpec((half, ct), lambda j, pos: (0, j)),
        ),
        **_params(cost_estimate=pl.CostEstimate(flops=2 * k * half * c, bytes_accessed=2 * k * (half + c), transcendentals=0)),
    )(pos, a, g, dep)


def mine(pos, a, g, r, dep, n, c0, c):
    k, d = a.shape[2:]
    half, quarter, ct = d // 2, d // 4, min(c, 512)

    def body(pos, a_ref, g_ref, r_ref, dep_ref, send_ref, own_ref):
        s = _dot(a_ref[0, 0], g_ref[0, 0]) + r_ref[...].astype(jnp.float32)
        first, second = s[:quarter], s[quarter:]
        on_first = pos[1] == 0
        own_ref[...] = jnp.where(on_first, first, second)
        send_ref[...] = jnp.where(on_first, second, first).astype(send_ref.dtype)

    return pl.pallas_call(
        body,
        out_shape=(
            jax.ShapeDtypeStruct((quarter, c), jnp.bfloat16),
            jax.ShapeDtypeStruct((quarter, c), jnp.float32),
        ),
        grid_spec=pltpu.PrefetchScalarGridSpec(
            num_scalar_prefetch=1,
            grid=(c // ct,),
            in_specs=[
                pl.BlockSpec((1, 1, k, half), lambda j, pos: (0, n, 0, pos[0])),
                pl.BlockSpec((1, 1, k, ct), lambda j, pos: (0, n, 0, c0 // ct + j)),
                pl.BlockSpec((half, ct), lambda j, pos: (0, j)),
                ANY,
            ],
            out_specs=(
                pl.BlockSpec((quarter, ct), lambda j, pos: (0, j)),
                pl.BlockSpec((quarter, ct), lambda j, pos: (0, j)),
            ),
        ),
        **_params(cost_estimate=pl.CostEstimate(flops=2 * k * half * c, bytes_accessed=2 * k * (half + c), transcendentals=0)),
    )(pos, a, g, r, dep)


def finish(pos, own, got, out, dep, shape, n, c0, c):
    quarter, ct = own.shape[0], min(c, 512)

    def body(pos, own_ref, got_ref, dep_ref, *rest):
        f_ref, o_ref = rest[-2:]
        f = (own_ref[...] + got_ref[...].astype(jnp.float32)).astype(f_ref.dtype)
        f_ref[...] = f
        o_ref[0] = f

    extra = () if out is None else (out,)
    return pl.pallas_call(
        body,
        out_shape=(jax.ShapeDtypeStruct((quarter, c), jnp.bfloat16), jax.ShapeDtypeStruct(shape, jnp.bfloat16)),
        grid_spec=pltpu.PrefetchScalarGridSpec(
            num_scalar_prefetch=1,
            grid=(c // ct,),
            in_specs=[pl.BlockSpec((quarter, ct), lambda j, pos: (0, j))] * 2 + [ANY] * (1 + len(extra)),
            out_specs=(
                pl.BlockSpec((quarter, ct), lambda j, pos: (0, j)),
                pl.BlockSpec((1, quarter, ct), lambda j, pos: (n, 2 * pos[0] + pos[1], c0 // ct + j)),
            ),
        ),
        input_output_aliases={4: 1} if extra else {},
        **_params(cost_estimate=pl.CostEstimate(flops=quarter * c * 600, bytes_accessed=quarter * c * 10, transcendentals=0)),
    )(pos, own, got, dep, *extra)


def place(pos, parts, out, dep, n, c0, c):
    quarter, ct = parts[0].shape[0], min(c, 512)
    tiles = c // ct

    def body(pos, z_ref, cf_ref, cz_ref, dep_ref, out_ref, o_ref):
        for s, ref in enumerate((z_ref, cf_ref, cz_ref)):
            @pl.when(pl.program_id(0) == s)
            def _():
                o_ref[0] = ref[...]

    def at(s):
        return lambda p, j, pos: (0, jnp.where(p == s, j, jnp.where(p < s, 0, tiles - 1)))

    def to(p, j, pos):
        core, x = jnp.where(p == 0, pos[0], 1 - pos[0]), jnp.where(p == 1, pos[1], 1 - pos[1])
        return n, 2 * core + x, c0 // ct + j

    return pl.pallas_call(
        body,
        out_shape=jax.ShapeDtypeStruct(out.shape, out.dtype),
        grid_spec=pltpu.PrefetchScalarGridSpec(
            num_scalar_prefetch=1,
            grid=(3, tiles),
            in_specs=[pl.BlockSpec((quarter, ct), at(s)) for s in range(3)] + [ANY] * 2,
            out_specs=pl.BlockSpec((1, quarter, ct), to),
        ),
        input_output_aliases={5: 0},
        **_params(cost_estimate=pl.CostEstimate(flops=quarter * c * 600, bytes_accessed=quarter * c * 12, transcendentals=0)),
    )(pos, *parts, dep, out)


def solution(mesh):
    over_x = [(0, 2), (2, 0), (1, 3), (3, 1)]
    over_core = [(0, 1), (1, 0), (2, 3), (3, 2)]

    def swap_x(t):
        return lax.ppermute(t, "dp", over_x)

    def swap_core(t):
        return lax.ppermute(t, "dp", over_core)

    def body(a, g):
        me = lax.axis_index("dp")
        pos = jnp.stack([lax.rem(me, 2), lax.div(me, 2)]).astype(jnp.int32)
        _, matrices, _, d = a.shape
        shape = (matrices, d, g.shape[3])
        chunks = []
        for n, widths in enumerate(WIDTHS):
            c0 = 0
            for c in widths:
                chunks.append((n, c0, c))
                c0 += c
        last = len(chunks)
        r, own, y, f, cf, z = {}, {}, {}, {}, {}, {}
        state = {"dep": pos, "out": None}

        def do_theirs(i):
            if i < last:
                t = theirs(pos, a, g, state["dep"], *chunks[i])
                state["dep"] = t
                r[i] = swap_core(t)

        def do_mine(i):
            send, own[i] = mine(pos, a, g, r[i], state["dep"], *chunks[i])
            state["dep"] = send
            y[i] = swap_x(send)

        def do_finish(i):
            f[i], state["out"] = finish(pos, own[i], y[i], state["out"], state["dep"], shape, *chunks[i])
            state["dep"] = f[i]
            z[i] = swap_x(f[i])
            cf[i] = swap_core(f[i])

        def do_place(i):
            cz = swap_core(z[i])
            state["out"] = place(pos, (z[i], cf[i], cz), state["out"], state["dep"], *chunks[i])

        do_theirs(0)
        for i in range(last):
            do_theirs(i + 1)
            do_mine(i)
            if i >= F_LAG:
                do_finish(i - F_LAG)
        for i in range(last - F_LAG, last):
            do_finish(i)
        for i in range(last):
            do_place(i)
        return state["out"]

    spec = P(("rep", "dp"))
    return jax.shard_map(body, mesh=mesh, in_specs=(spec, spec), out_specs=P("rep"), check_vma=False)
```

time: 1680 us -> 763 us (0.45)
  blocking collectives: 1480 us -> 0 us
  Pallas kernels: 0 us -> 488 us
  waiting for transfers between devices: 0 us -> 224 us
  matrix products: 199 us -> 0 us
  starting transfers between devices: 0 us -> 40.3 us
    dot_general x1 -> x0, blocking collectives: 1480 us -> none  [step(): jnp.einsum('rsntd,rsntf->rndf', a, g, preferred_element_type=jnp.float32)]
    pallas_call x0 -> x56, Pallas kernels: none -> 488 us  [the longest x14 180 us: mine(): pl.pallas_call(body, out_shape=(jax.ShapeDtypeStruct((quarter, c), jnp.bf...]
    ppermute x0 -> x70, waiting for transfers between devices: none -> 224 us  [the longest x28 220 us: swap_x(): return lax.ppermute(t, 'dp', over_x)]
    dot_general x1 -> x0, matrix products: 199 us -> none  [step(): jnp.einsum('rsntd,rsntf->rndf', a, g, preferred_element_type=jnp.float32)]
    ppermute x0 -> x70, starting transfers between devices: none -> 40.3 us  [the longest x28 32.3 us: swap_x(): return lax.ppermute(t, 'dp', over_x)]
  transfers between devices with their start and end apart: 0 -> 70, of which waited for: 0 -> 16; matrix products, arithmetic and copies ran while one was open for 0% -> 0% of each run, Pallas kernels for 0% -> 63%
where the time goes in v1:
time: 763 us; the launch traced here: 754 us
  Pallas kernels  488 us (64%)
  waiting for transfers between devices  224 us (29%)
  starting transfers between devices  40.3 us (5%)
    ppermute x28, waiting for transfers between devices, swap_x(): return lax.ppermute(t, 'dp', over_x)  220 us
    pallas_call x14, Pallas kernels, mine(): pl.pallas_call(body, out_shape=(jax.ShapeDtypeStruct((quarter, c), jnp.bf...  180 us
    pallas_call x14, Pallas kernels, theirs(): pl.pallas_call(body, out_shape=jax.ShapeDtypeStruct((half, c), jnp.bfloat...  174 us
    pallas_call x14, Pallas kernels, place(): pl.pallas_call(body, out_shape=jax.ShapeDtypeStruct(out.shape, out.dtype)...  81.9 us
    pallas_call x14, Pallas kernels, finish(): pl.pallas_call(body, out_shape=(jax.ShapeDtypeStruct((quarter, c), jnp.bf...  51.8 us
    ppermute x28, starting transfers between devices, swap_x(): return lax.ppermute(t, 'dp', over_x)  32.3 us
  transfers between devices with their start and end apart: 70, of which 16 were waited for; matrix products, arithmetic and copies ran while one was open for 0% of the time, Pallas kernels for 63%

profile of v1, /device:TPU:0, one launch (start us, length us, event | category | flops | bytes accessed | tf_op | source)
XLA Modules:
  0.0 753.5 jit_solution(7123029176174619024)
XLA Ops:
  38.0 12.8 %shard_map.33.dep_ref = bf16[768,1024]{1,0:T(8,128)(2,1)} custom-call(s32[2]{0:T(128)} %pad_add_fusion.pos.dep_ref, bf16[1,4,4096,1536]{3,2,1,0:T(8,128)(2,1)} %a_ref.55, bf16[1,4,4096,3584]{3,2,1,0:T(8,128)(2,1)} %g_ref.55, bf16[384,256]{1,0:T(8,128)(2,1)} %get-tuple-element.62.dep_ref), custom_call_target="tpu_custom_call" | custom-call | flops 6442450944 | bytes 14680064 | tf_op jit(solution)/shard_map/pallas_call | solution.py:35
  63.3 16.0 %shard_map.35.dep_ref = bf16[768,1536]{1,0:T(8,128)(2,1)} custom-call(s32[2]{0:T(128)} %pad_add_fusion.pos.dep_ref, bf16[1,4,4096,1536]{3,2,1,0:T(8,128)(2,1)} %a_ref.55, bf16[1,4,4096,3584]{3,2,1,0:T(8,128)(2,1)} %g_ref.55, bf16[384,512]{1,0:T(8,128)(2,1)} %get-tuple-element.63.dep_ref), custom_call_target="tpu_custom_call" | custom-call | flops 9663676416 | bytes 18874368 | tf_op jit(solution)/shard_map/pallas_call | solution.py:35
  79.3 13.1 %shard_map.36 = (bf16[384,1024]{1,0:T(8,128)(2,1)}, f32[384,1024]{1,0:T(8,128)}) custom-call(s32[2]{0:T(128)} %pad_add_fusion.pos.dep_ref, bf16[1,4,4096,1536]{3,2,1,0:T(8,128)(2,1)} %a_ref.55, bf16[1,4,4096,3584]{3,2,1,0:T(8,128)(2,1)} %g_ref.55, bf16[768,1024]{1,0:T(8,128)(2,1)} %collective-permute-done.2.r_ref, bf16[768,1536]{1,0:T(8,128)(2,1)} %shard_map.35.dep_ref), custom_call_target="tpu_custom_call" | custom-call | flops 6442450944 | bytes 14680064 | tf_op jit(solution)/shard_map/pallas_call | solution.py:63
  95.0 19.5 %shard_map.38.dep_ref = bf16[768,2048]{1,0:T(8,128)(2,1)} custom-call(s32[2]{0:T(128)} %pad_add_fusion.pos.dep_ref, bf16[1,4,4096,1536]{3,2,1,0:T(8,128)(2,1)} %a_ref.55, bf16[1,4,4096,3584]{3,2,1,0:T(8,128)(2,1)} %g_ref.55, bf16[384,256]{1,0:T(8,128)(2,1)} %get-tuple-element.68.dep_ref), custom_call_target="tpu_custom_call" | custom-call | flops 12884901888 | bytes 23068672 | tf_op jit(solution)/shard_map/pallas_call | solution.py:35
  116.9 17.1 %shard_map.39 = (bf16[384,1536]{1,0:T(8,128)(2,1)}, f32[384,1536]{1,0:T(8,128)}) custom-call(s32[2]{0:T(128)} %pad_add_fusion.pos.dep_ref, bf16[1,4,4096,1536]{3,2,1,0:T(8,128)(2,1)} %a_ref.55, bf16[1,4,4096,3584]{3,2,1,0:T(8,128)(2,1)} %g_ref.55, bf16[768,1536]{1,0:T(8,128)(2,1)} %collective-permute-done.6.r_ref, bf16[768,2048]{1,0:T(8,128)(2,1)} %shard_map.38.dep_ref), custom_call_target="tpu_custom_call" | custom-call | flops 9663676416 | bytes 18874368 | tf_op jit(solution)/shard_map/pallas_call | solution.py:63
  136.5 16.1 %shard_map.41.dep_ref = bf16[768,1536]{1,0:T(8,128)(2,1)} custom-call(s32[2]{0:T(128)} %pad_add_fusion.pos.dep_ref, bf16[1,4,4096,1536]{3,2,1,0:T(8,128)(2,1)} %a_ref.55, bf16[1,4,4096,3584]{3,2,1,0:T(8,128)(2,1)} %g_ref.55, bf16[384,256]{1,0:T(8,128)(2,1)} %get-tuple-element.71.dep_ref), custom_call_target="tpu_custom_call" | custom-call | flops 9663676416 | bytes 18874368 | tf_op jit(solution)/shard_map/pallas_call | solution.py:35
  152.7 20.3 %shard_map.42 = (bf16[384,2048]{1,0:T(8,128)(2,1)}, f32[384,2048]{1,0:T(8,128)}) custom-call(s32[2]{0:T(128)} %pad_add_fusion.pos.dep_ref, bf16[1,4,4096,1536]{3,2,1,0:T(8,128)(2,1)} %a_ref.55, bf16[1,4,4096,3584]{3,2,1,0:T(8,128)(2,1)} %g_ref.55, bf16[768,2048]{1,0:T(8,128)(2,1)} %collective-permute-done.10.r_ref, bf16[768,1536]{1,0:T(8,128)(2,1)} %shard_map.41.dep_ref), custom_call_target="tpu_custom_call" | custom-call | flops 12884901888 | bytes 23068672 | tf_op jit(solution)/shard_map/pallas_call | solution.py:63
  175.8 19.5 %shard_map.44.dep_ref = bf16[768,2048]{1,0:T(8,128)(2,1)} custom-call(s32[2]{0:T(128)} %pad_add_fusion.pos.dep_ref, bf16[1,4,4096,1536]{3,2,1,0:T(8,128)(2,1)} %a_ref.55, bf16[1,4,4096,3584]{3,2,1,0:T(8,128)(2,1)} %g_ref.55, bf16[384,512]{1,0:T(8,128)(2,1)} %get-tuple-element.75.dep_ref), custom_call_target="tpu_custom_call" | custom-call | flops 12884901888 | bytes 23068672 | tf_op jit(solution)/shard_map/pallas_call | solution.py:35
  203.9 16.7 %shard_map.45 = (bf16[384,1536]{1,0:T(8,128)(2,1)}, f32[384,1536]{1,0:T(8,128)}) custom-call(s32[2]{0:T(128)} %pad_add_fusion.pos.dep_ref, bf16[1,4,4096,1536]{3,2,1,0:T(8,128)(2,1)} %a_ref.55, bf16[1,4,4096,3584]{3,2,1,0:T(8,128)(2,1)} %g_ref.55, bf16[768,1536]{1,0:T(8,128)(2,1)} %collective-permute-done.8.r_ref, bf16[768,2048]{1,0:T(8,128)(2,1)} %shard_map.44.dep_ref), custom_call_target="tpu_custom_call" | custom-call | flops 9663676416 | bytes 18874368 | tf_op jit(solution)/shard_map/pallas_call | solution.py:63
  225.9 16.2 %shard_map.47.dep_ref = bf16[768,1536]{1,0:T(8,128)(2,1)} custom-call(s32[2]{0:T(128)} %pad_add_fusion.pos.dep_ref, bf16[1,4,4096,1536]{3,2,1,0:T(8,128)(2,1)} %a_ref.55, bf16[1,4,4096,3584]{3,2,1,0:T(8,128)(2,1)} %g_ref.55, bf16[384,1024]{1,0:T(8,128)(2,1)} %get-tuple-element.78.dep_ref), custom_call_target="tpu_custom_call" | custom-call | flops 9663676416 | bytes 18874368 | tf_op jit(solution)/shard_map/pallas_call | solution.py:35
  251.8 20.2 %shard_map.48 = (bf16[384,2048]{1,0:T(8,128)(2,1)}, f32[384,2048]{1,0:T(8,128)}) custom-call(s32[2]{0:T(128)} %pad_add_fusion.pos.dep_ref, bf16[1,4,4096,1536]{3,2,1,0:T(8,128)(2,1)} %a_ref.55, bf16[1,4,4096,3584]{3,2,1,0:T(8,128)(2,1)} %g_ref.55, bf16[768,2048]{1,0:T(8,128)(2,1)} %collective-permute-done.13.r_ref, bf16[768,1536]{1,0:T(8,128)(2,1)} %shard_map.47.dep_ref), custom_call_target="tpu_custom_call" | custom-call | flops 12884901888 | bytes 23068672 | tf_op jit(solution)/shard_map/pallas_call | solution.py:63
  276.8 18.0 %collective-permute-done.61.z_ref = bf16[384,512]{1,0:T(8,128)(2,1)} collective-permute-done((bf16[384,512]{1,0:T(8,128)(2,1)}, bf16[384,512]{1,0:T(8,128)(2,1)}, u32[]{:S(2)}, u32[]{:S(2)}) %collective-permute-start.61) | collective-permute-done | bytes 393248 | tf_op jit(solution)/shard_map/ppermute | solution.py:150
  295.3 16.1 %shard_map.50.dep_ref = bf16[768,1536]{1,0:T(8,128)(2,1)} custom-call(s32[2]{0:T(128)} %pad_add_fusion.pos.dep_ref, bf16[1,4,4096,1536]{3,2,1,0:T(8,128)(2,1)} %a_ref.55, bf16[1,4,4096,3584]{3,2,1,0:T(8,128)(2,1)} %g_ref.55, bf16[384,1536]{1,0:T(8,128)(2,1)} %get-tuple-element.82.dep_ref), custom_call_target="tpu_custom_call" | custom-call | flops 9663676416 | bytes 18874368 | tf_op jit(solution)/shard_map/pallas_call | solution.py:35
  317.4 16.8 %shard_map.51 = (bf16[384,1536]{1,0:T(8,128)(2,1)}, f32[384,1536]{1,0:T(8,128)}) custom-call(s32[2]{0:T(128)} %pad_add_fusion.pos.dep_ref, bf16[1,4,4096,1536]{3,2,1,0:T(8,128)(2,1)} %a_ref.55, bf16[1,4,4096,3584]{3,2,1,0:T(8,128)(2,1)} %g_ref.55, bf16[768,1536]{1,0:T(8,128)(2,1)} %collective-permute-done.11.r_ref, bf16[768,1536]{1,0:T(8,128)(2,1)} %shard_map.50.dep_ref), custom_call_target="tpu_custom_call" | custom-call | flops 9663676416 | bytes 18874368 | tf_op jit(solution)/shard_map/pallas_call | solution.py:63
  339.3 12.8 %shard_map.53.dep_ref = bf16[768,1024]{1,0:T(8,128)(2,1)} custom-call(s32[2]{0:T(128)} %pad_add_fusion.pos.dep_ref, bf16[1,4,4096,1536]{3,2,1,0:T(8,128)(2,1)} %a_ref.55, bf16[1,4,4096,3584]{3,2,1,0:T(8,128)(2,1)} %g_ref.55, bf16[384,2048]{1,0:T(8,128)(2,1)} %get-tuple-element.88.dep_ref), custom_call_target="tpu_custom_call" | custom-call | flops 6442450944 | bytes 14680064 | tf_op jit(solution)/shard_map/pallas_call | solution.py:35
  352.2 47.7 %collective-permute-done.55.z_ref = bf16[384,1536]{1,0:T(8,128)(2,1)} collective-permute-done((bf16[384,1536]{1,0:T(8,128)(2,1)}, bf16[384,1536]{1,0:T(8,128)(2,1)}, u32[]{:S(2)}, u32[]{:S(2)}) %collective-permute-start.55) | collective-permute-done | bytes 1179680 | tf_op jit(solution)/shard_map/ppermute | solution.py:150
  401.8 16.7 %shard_map.54 = (bf16[384,1536]{1,0:T(8,128)(2,1)}, f32[384,1536]{1,0:T(8,128)}) custom-call(s32[2]{0:T(128)} %pad_add_fusion.pos.dep_ref, bf16[1,4,4096,1536]{3,2,1,0:T(8,128)(2,1)} %a_ref.55, bf16[1,4,4096,3584]{3,2,1,0:T(8,128)(2,1)} %g_ref.55, bf16[768,1536]{1,0:T(8,128)(2,1)} %collective-permute-done.16.r_ref, bf16[768,1024]{1,0:T(8,128)(2,1)} %shard_map.53.dep_ref), custom_call_target="tpu_custom_call" | custom-call | flops 9663676416 | bytes 18874368 | tf_op jit(solution)/shard_map/pallas_call | solution.py:63
  434.1 13.1 %shard_map.57 = (bf16[384,1024]{1,0:T(8,128)(2,1)}, f32[384,1024]{1,0:T(8,128)}) custom-call(s32[2]{0:T(128)} %pad_add_fusion.pos.dep_ref, bf16[1,4,4096,1536]{3,2,1,0:T(8,128)(2,1)} %a_ref.55, bf16[1,4,4096,3584]{3,2,1,0:T(8,128)(2,1)} %g_ref.55, bf16[768,1024]{1,0:T(8,128)(2,1)} %collective-permute-done.20.r_ref, bf16[768,512]{1,0:T(8,128)(2,1)} %shard_map.56.dep_ref), custom_call_target="tpu_custom_call" | custom-call | flops 6442450944 | bytes 14680064 | tf_op jit(solution)/shard_map/pallas_call | solution.py:63
  493.3 41.8 %collective-permute-done.25.got_ref = bf16[384,256]{1,0:T(8,128)(2,1)} collective-permute-done((bf16[384,256]{1,0:T(8,128)(2,1)}, bf16[384,256]{1,0:T(8,128)(2,1)}, u32[]{:S(2)}, u32[]{:S(2)}) %collective-permute-start.25) | collective-permute-done | bytes 196640 | tf_op jit(solution)/shard_map/ppermute | solution.py:150
  552.7 24.4 %collective-permute-done.26.got_ref = bf16[384,512]{1,0:T(8,128)(2,1)} collective-permute-done((bf16[384,512]{1,0:T(8,128)(2,1)}, bf16[384,512]{1,0:T(8,128)(2,1)}, u32[]{:S(2)}, u32[]{:S(2)}) %collective-permute-start.26) | collective-permute-done | bytes 393248 | tf_op jit(solution)/shard_map/ppermute | solution.py:150
  587.7 18.9 %collective-permute-done.24.got_ref = bf16[384,256]{1,0:T(8,128)(2,1)} collective-permute-done((bf16[384,256]{1,0:T(8,128)(2,1)}, bf16[384,256]{1,0:T(8,128)(2,1)}, u32[]{:S(2)}, u32[]{:S(2)}) %collective-permute-start.24) | collective-permute-done | bytes 196640 | tf_op jit(solution)/shard_map/ppermute | solution.py:150
  624.3 27.5 %collective-permute-done.28.z_ref = bf16[384,256]{1,0:T(8,128)(2,1)} collective-permute-done((bf16[384,256]{1,0:T(8,128)(2,1)}, bf16[384,256]{1,0:T(8,128)(2,1)}, u32[]{:S(2)}, u32[]{:S(2)}) %collective-permute-start.28) | collective-permute-done | bytes 196640 | tf_op jit(solution)/shard_map/ppermute | solution.py:150
  652.3 14.5 %collective-permute-done.37.z_ref = bf16[384,1024]{1,0:T(8,128)(2,1)} collective-permute-done((bf16[384,1024]{1,0:T(8,128)(2,1)}, bf16[384,1024]{1,0:T(8,128)(2,1)}, u32[]{:S(2)}, u32[]{:S(2)}) %collective-permute-start.37) | collective-permute-done | bytes 786464 | tf_op jit(solution)/shard_map/ppermute | solution.py:150
  712.1 9.8 %shard_map.77.out_ref = bf16[4,1536,3584]{2,1,0:T(8,128)(2,1)} custom-call(s32[2]{0:T(128)} %pad_add_fusion.pos.dep_ref, bf16[384,2048]{1,0:T(8,128)(2,1)} %collective-permute-done.46.z_ref, bf16[384,2048]{1,0:T(8,128)(2,1)} %collective-permute-done.47.cf_ref, bf16[384,2048]{1,0:T(8,128)(2,1)} %collective-permute-done.48.cz_ref, ...), custom_call_target="tpu_custom_call", output_to_operand_aliasing={{}: (5, {})} | custom-call | flops 471859200 | bytes 9437184 | tf_op jit(solution)/shard_map/pallas_call | solution.py:131
  (173 shorter events, 287.5 us)
Async XLA Ops:
  114.9 58.0 %collective-permute-start.9 = (bf16[384,512]{1,0:T(8,128)(2,1)}, bf16[384,512]{1,0:T(8,128)(2,1)}, u32[]{:S(2)}, u32[]{:S(2)}) collective-permute-start(bf16[384,512]{1,0:T(8,128)(2,1)} %get-tuple-element.63.dep_ref), channel_id=1, source_target_pairs={{0,2},{2,0},{1,3},{3,1},{4,6},{6,4},{5,7},{7,5}} | collective-permute-start | bytes 1179656 | tf_op jit(solution)/shard_map/ppermute | solution.py:150
  195.3 56.0 %collective-permute-start.13 = (bf16[768,2048]{1,0:T(8,128)(2,1)}, bf16[768,2048]{1,0:T(8,128)(2,1)}, u32[]{:S(2)}, u32[]{:S(2)}) collective-permute-start(bf16[768,2048]{1,0:T(8,128)(2,1)} %shard_map.44.dep_ref), channel_id=1, source_target_pairs={{0,1},{1,0},{2,3},{3,2},{4,5},{5,4},{6,7},{7,6}} | collective-permute-start | bytes 9437192 | tf_op jit(solution)/shard_map/ppermute | solution.py:153
  249.3 62.4 %collective-permute-start.17 = (bf16[384,2048]{1,0:T(8,128)(2,1)}, bf16[384,2048]{1,0:T(8,128)(2,1)}, u32[]{:S(2)}, u32[]{:S(2)}) collective-permute-start(bf16[384,2048]{1,0:T(8,128)(2,1)} %get-tuple-element.73.dep_ref), channel_id=1, source_target_pairs={{0,2},{2,0},{1,3},{3,1},{4,6},{6,4},{5,7},{7,5}} | collective-permute-start | bytes 4718600 | tf_op jit(solution)/shard_map/ppermute | solution.py:150
  251.3 64.1 %collective-permute-start.11 = (bf16[768,1536]{1,0:T(8,128)(2,1)}, bf16[768,1536]{1,0:T(8,128)(2,1)}, u32[]{:S(2)}, u32[]{:S(2)}) collective-permute-start(bf16[768,1536]{1,0:T(8,128)(2,1)} %shard_map.47.dep_ref), channel_id=1, source_target_pairs={{0,1},{1,0},{2,3},{3,2},{4,5},{5,4},{6,7},{7,6}} | collective-permute-start | bytes 7077896 | tf_op jit(solution)/shard_map/ppermute | solution.py:153
  311.4 90.2 %collective-permute-start.16 = (bf16[768,1536]{1,0:T(8,128)(2,1)}, bf16[768,1536]{1,0:T(8,128)(2,1)}, u32[]{:S(2)}, u32[]{:S(2)}) collective-permute-start(bf16[768,1536]{1,0:T(8,128)(2,1)} %shard_map.50.dep_ref), channel_id=1, source_target_pairs={{0,1},{1,0},{2,3},{3,2},{4,5},{5,4},{6,7},{7,6}} | collective-permute-start | bytes 7077896 | tf_op jit(solution)/shard_map/ppermute | solution.py:153
  315.3 84.5 %collective-permute-start.19 = (bf16[384,2048]{1,0:T(8,128)(2,1)}, bf16[384,2048]{1,0:T(8,128)(2,1)}, u32[]{:S(2)}, u32[]{:S(2)}) collective-permute-start(bf16[384,2048]{1,0:T(8,128)(2,1)} %get-tuple-element.80.dep_ref), channel_id=1, source_target_pairs={{0,2},{2,0},{1,3},{3,1},{4,6},{6,4},{5,7},{7,5}} | collective-permute-start | bytes 4718600 | tf_op jit(solution)/shard_map/ppermute | solution.py:150
  315.4 84.5 %collective-permute-start.55 = (bf16[384,1536]{1,0:T(8,128)(2,1)}, bf16[384,1536]{1,0:T(8,128)(2,1)}, u32[]{:S(2)}, u32[]{:S(2)}) collective-permute-start(bf16[384,1536]{1,0:T(8,128)(2,1)} %get-tuple-element.82.dep_ref), channel_id=1, source_target_pairs={{0,2},{2,0},{1,3},{3,1},{4,6},{6,4},{5,7},{7,5}} | collective-permute-start | bytes 3538952 | tf_op jit(solution)/shard_map/ppermute | solution.py:150
  352.1 81.5 %collective-permute-start.52 = (bf16[384,2048]{1,0:T(8,128)(2,1)}, bf16[384,2048]{1,0:T(8,128)(2,1)}, u32[]{:S(2)}, u32[]{:S(2)}) collective-permute-start(bf16[384,2048]{1,0:T(8,128)(2,1)} %get-tuple-element.88.dep_ref), channel_id=1, source_target_pairs={{0,2},{2,0},{1,3},{3,1},{4,6},{6,4},{5,7},{7,5}} | collective-permute-start | bytes 4718600 | tf_op jit(solution)/shard_map/ppermute | solution.py:150
  352.1 81.4 %collective-permute-start.20 = (bf16[768,1024]{1,0:T(8,128)(2,1)}, bf16[768,1024]{1,0:T(8,128)(2,1)}, u32[]{:S(2)}, u32[]{:S(2)}) collective-permute-start(bf16[768,1024]{1,0:T(8,128)(2,1)} %shard_map.53.dep_ref), channel_id=1, source_target_pairs={{0,1},{1,0},{2,3},{3,2},{4,5},{5,4},{6,7},{7,6}} | collective-permute-start | bytes 4718600 | tf_op jit(solution)/shard_map/ppermute | solution.py:153
  399.8 59.2 %collective-permute-start.14 = (bf16[384,1536]{1,0:T(8,128)(2,1)}, bf16[384,1536]{1,0:T(8,128)(2,1)}, u32[]{:S(2)}, u32[]{:S(2)}) collective-permute-start(bf16[384,1536]{1,0:T(8,128)(2,1)} %get-tuple-element.84.dep_ref), channel_id=1, source_target_pairs={{0,2},{2,0},{1,3},{3,1},{4,6},{6,4},{5,7},{7,5}} | collective-permute-start | bytes 3538952 | tf_op jit(solution)/shard_map/ppermute | solution.py:150
  401.6 57.9 %collective-permute-start.53 = (bf16[384,2048]{1,0:T(8,128)(2,1)}, bf16[384,2048]{1,0:T(8,128)(2,1)}, u32[]{:S(2)}, u32[]{:S(2)}) collective-permute-start(bf16[384,2048]{1,0:T(8,128)(2,1)} %get-tuple-element.88.dep_ref), channel_id=1, source_target_pairs={{0,1},{1,0},{2,3},{3,2},{4,5},{5,4},{6,7},{7,6}} | collective-permute-start | bytes 4718600 | tf_op jit(solution)/shard_map/ppermute | solution.py:153
  433.5 59.7 %collective-permute-start.54 = (bf16[384,2048]{1,0:T(8,128)(2,1)}, bf16[384,2048]{1,0:T(8,128)(2,1)}, u32[]{:S(2)}, u32[]{:S(2)}) collective-permute-start(bf16[384,2048]{1,0:T(8,128)(2,1)} %collective-permute-done.52.z_ref), channel_id=1, source_target_pairs={{0,1},{1,0},{2,3},{3,2},{4,5},{5,4},{6,7},{7,6}} | collective-permute-start | bytes 4718600 | tf_op jit(solution)/shard_map/ppermute | solution.py:153
  461.3 73.7 %collective-permute-start.22 = (bf16[384,1536]{1,0:T(8,128)(2,1)}, bf16[384,1536]{1,0:T(8,128)(2,1)}, u32[]{:S(2)}, u32[]{:S(2)}) collective-permute-start(bf16[384,1536]{1,0:T(8,128)(2,1)} %get-tuple-element.89.dep_ref), channel_id=1, source_target_pairs={{0,2},{2,0},{1,3},{3,1},{4,6},{6,4},{5,7},{7,5}} | collective-permute-start | bytes 3538952 | tf_op jit(solution)/shard_map/ppermute | solution.py:150
  463.0 72.6 %collective-permute-start.49 = (bf16[384,1536]{1,0:T(8,128)(2,1)}, bf16[384,1536]{1,0:T(8,128)(2,1)}, u32[]{:S(2)}, u32[]{:S(2)}) collective-permute-start(bf16[384,1536]{1,0:T(8,128)(2,1)} %get-tuple-element.91.dep_ref), channel_id=1, source_target_pairs={{0,2},{2,0},{1,3},{3,1},{4,6},{6,4},{5,7},{7,5}} | collective-permute-start | bytes 3538952 | tf_op jit(solution)/shard_map/ppermute | solution.py:150
  492.9 118.8 %collective-permute-start.46 = (bf16[384,2048]{1,0:T(8,128)(2,1)}, bf16[384,2048]{1,0:T(8,128)(2,1)}, u32[]{:S(2)}, u32[]{:S(2)}) collective-permute-start(bf16[384,2048]{1,0:T(8,128)(2,1)} %get-tuple-element.95.dep_ref), channel_id=1, source_target_pairs={{0,2},{2,0},{1,3},{3,1},{4,6},{6,4},{5,7},{7,5}} | collective-permute-start | bytes 4718600 | tf_op jit(solution)/shard_map/ppermute | solution.py:150
  493.3 94.2 %collective-permute-start.50 = (bf16[384,1536]{1,0:T(8,128)(2,1)}, bf16[384,1536]{1,0:T(8,128)(2,1)}, u32[]{:S(2)}, u32[]{:S(2)}) collective-permute-start(bf16[384,1536]{1,0:T(8,128)(2,1)} %get-tuple-element.91.dep_ref), channel_id=1, source_target_pairs={{0,1},{1,0},{2,3},{3,2},{4,5},{5,4},{6,7},{7,6}} | collective-permute-start | bytes 3538952 | tf_op jit(solution)/shard_map/ppermute | solution.py:153
  535.0 76.7 %collective-permute-start.47 = (bf16[384,2048]{1,0:T(8,128)(2,1)}, bf16[384,2048]{1,0:T(8,128)(2,1)}, u32[]{:S(2)}, u32[]{:S(2)}) collective-permute-start(bf16[384,2048]{1,0:T(8,128)(2,1)} %get-tuple-element.95.dep_ref), channel_id=1, source_target_pairs={{0,1},{1,0},{2,3},{3,2},{4,5},{5,4},{6,7},{7,6}} | collective-permute-start | bytes 4718600 | tf_op jit(solution)/shard_map/ppermute | solution.py:153
  539.3 112.4 %collective-permute-start.43 = (bf16[384,1536]{1,0:T(8,128)(2,1)}, bf16[384,1536]{1,0:T(8,128)(2,1)}, u32[]{:S(2)}, u32[]{:S(2)}) collective-permute-start(bf16[384,1536]{1,0:T(8,128)(2,1)} %get-tuple-element.98.dep_ref), channel_id=1, source_target_pairs={{0,2},{2,0},{1,3},{3,1},{4,6},{6,4},{5,7},{7,5}} | collective-permute-start | bytes 3538952 | tf_op jit(solution)/shard_map/ppermute | solution.py:150
  611.7 55.6 %collective-permute-start.40 = (bf16[384,1536]{1,0:T(8,128)(2,1)}, bf16[384,1536]{1,0:T(8,128)(2,1)}, u32[]{:S(2)}, u32[]{:S(2)}) collective-permute-start(bf16[384,1536]{1,0:T(8,128)(2,1)} %get-tuple-element.102.dep_ref), channel_id=1, source_target_pairs={{0,2},{2,0},{1,3},{3,1},{4,6},{6,4},{5,7},{7,5}} | collective-permute-start | bytes 3538952 | tf_op jit(solution)/shard_map/ppermute | solution.py:150
  670.0 73.2 %collective-permute-start.36 = (bf16[384,512]{1,0:T(8,128)(2,1)}, bf16[384,512]{1,0:T(8,128)(2,1)}, u32[]{:S(2)}, u32[]{:S(2)}) collective-permute-start(bf16[384,512]{1,0:T(8,128)(2,1)} %collective-permute-done.34.z_ref), channel_id=1, source_target_pairs={{0,1},{1,0},{2,3},{3,2},{4,5},{5,4},{6,7},{7,6}} | collective-permute-start | bytes 1179656 | tf_op jit(solution)/shard_map/ppermute | solution.py:153
  693.6 53.1 %collective-permute-start.32 = (bf16[384,256]{1,0:T(8,128)(2,1)}, bf16[384,256]{1,0:T(8,128)(2,1)}, u32[]{:S(2)}, u32[]{:S(2)}) collective-permute-start(bf16[384,256]{1,0:T(8,128)(2,1)} %get-tuple-element.113.dep_ref), channel_id=1, source_target_pairs={{0,1},{1,0},{2,3},{3,2},{4,5},{5,4},{6,7},{7,6}} | collective-permute-start | bytes 589832 | tf_op jit(solution)/shard_map/ppermute | solution.py:153
  694.0 55.9 %collective-permute-start.29 = (bf16[384,256]{1,0:T(8,128)(2,1)}, bf16[384,256]{1,0:T(8,128)(2,1)}, u32[]{:S(2)}, u32[]{:S(2)}) collective-permute-start(bf16[384,256]{1,0:T(8,128)(2,1)} %get-tuple-element.115.dep_ref), channel_id=1, source_target_pairs={{0,1},{1,0},{2,3},{3,2},{4,5},{5,4},{6,7},{7,6}} | collective-permute-start | bytes 589832 | tf_op jit(solution)/shard_map/ppermute | solution.py:153
  694.2 52.5 %collective-permute-start.33 = (bf16[384,256]{1,0:T(8,128)(2,1)}, bf16[384,256]{1,0:T(8,128)(2,1)}, u32[]{:S(2)}, u32[]{:S(2)}) collective-permute-start(bf16[384,256]{1,0:T(8,128)(2,1)} %collective-permute-done.31.z_ref), channel_id=1, source_target_pairs={{0,1},{1,0},{2,3},{3,2},{4,5},{5,4},{6,7},{7,6}} | collective-permute-start | bytes 589832 | tf_op jit(solution)/shard_map/ppermute | solution.py:153
  694.5 55.4 %collective-permute-start.30 = (bf16[384,256]{1,0:T(8,128)(2,1)}, bf16[384,256]{1,0:T(8,128)(2,1)}, u32[]{:S(2)}, u32[]{:S(2)}) collective-permute-start(bf16[384,256]{1,0:T(8,128)(2,1)} %collective-permute-done.28.z_ref), channel_id=1, source_target_pairs={{0,1},{1,0},{2,3},{3,2},{4,5},{5,4},{6,7},{7,6}} | collective-permute-start | bytes 589832 | tf_op jit(solution)/shard_map/ppermute | solution.py:153
  (46 other events, 1335.8 us)

commit v2 on v0

v2 whole, which is shorter than its diff:
```python
import jax
import jax.numpy as jnp
from jax import lax
from jax.experimental import pallas as pl
from jax.experimental.pallas import tpu as pltpu
from jax.sharding import PartitionSpec as P


CT = 256
SENDS = 8
KEPT = 16
LAG = 8
PIECES = ((0, 0, 3584), (1, 0, 3584), (2, 0, 3584), (3, 0, 1536), (3, 1536, 1024), (3, 2560, 512), (3, 3072, 256), (3, 3328, 256))
VMEM = 67043328
ANY = pl.BlockSpec(memory_space=pl.ANY)
MESH = pl.DeviceIdType.MESH


def _dot(a, g):
    return lax.dot_general(a, g, (((0,), (0,)), ((), ())), preferred_element_type=jnp.float32)


def reduce_kernel(a, g, *refs):
    outs, scratch = refs[: len(PIECES)], refs[len(PIECES) :]
    abuf, gbuf, tsend, term, xsend, own, got, fbuf, a_sem, g_sem, ts_sem, tr_sem, xs_sem, xr_sem, f_sem = scratch
    _, matrices, _, d = a.shape
    half, quarter, per = d // 2, d // 4, g.shape[3] // CT
    tiles = matrices * per
    me = lax.axis_index("dp")
    core, x = lax.rem(me, 2), lax.div(me, 2)
    sibling, across = 2 * x + 1 - core, 2 * (1 - x) + core

    def load_a(n, side):
        first = pl.multiple_of(half * jnp.where(side == 0, 1 - core, core), half)
        s = lax.rem(n, 2)
        return pltpu.make_async_copy(a.at[0, n, :, pl.ds(first, half)], abuf.at[s, side], a_sem.at[s, side])

    def load_g(t):
        n, j = lax.div(t, per), lax.rem(t, per)
        s = lax.rem(t, 2)
        return pltpu.make_async_copy(g.at[0, n, :, pl.ds(pl.multiple_of(j * CT, CT), CT)], gbuf.at[s], g_sem.at[s])

    def send_term(t):
        s = lax.rem(t, 2)
        return pltpu.make_async_remote_copy(
            tsend.at[s], term.at[s], ts_sem.at[s], tr_sem.at[s], device_id={"dp": sibling}, device_id_type=MESH
        )

    def send_x(t):
        s = lax.rem(t, SENDS)
        return pltpu.make_async_remote_copy(
            xsend.at[s], got.at[t], xs_sem.at[s], xr_sem.at[t], device_id={"dp": across}, device_id_type=MESH
        )

    def store_f(u, out, c0):
        s = lax.rem(u, 2)
        at = pl.multiple_of(lax.rem(u, per) * CT - c0, CT)
        return pltpu.make_async_copy(fbuf.at[s], out.at[:, pl.ds(at, CT)], f_sem.at[s])

    def wait_f(u):
        s = lax.rem(u, 2)
        pltpu.make_async_copy(fbuf.at[s], outs[0].at[:, pl.ds(0, CT)], f_sem.at[s]).wait()

    def finish(u):
        send_x(u).wait_recv()

        @pl.when(u >= 2)
        def _():
            wait_f(u - 2)

        fbuf[lax.rem(u, 2)] = (own[lax.rem(u, KEPT)] + got[u].astype(jnp.float32)).astype(fbuf.dtype)
        for (n, c0, c), out in zip(PIECES, outs):
            lo = n * per + c0 // CT

            @pl.when((u >= lo) & (u < lo + c // CT))
            def _():
                store_f(u, out, c0).start()

    load_a(0, 0).start()
    load_g(0).start()
    barrier = pltpu.get_barrier_semaphore()
    for other in (sibling, across):
        pl.semaphore_signal(barrier, inc=1, device_id={"dp": other}, device_id_type=MESH)
    pl.semaphore_wait(barrier, 2)

    def step(t, _):
        n, j = lax.div(t, per), lax.rem(t, per)
        s, sa = lax.rem(t, 2), lax.rem(n, 2)

        @pl.when(j == 0)
        def _():
            load_a(n, 0).wait()

        load_g(t).wait()

        @pl.when(t == 0)
        def _():
            load_a(0, 1).start()

        @pl.when(t + 1 < tiles)
        def _():
            load_g(t + 1).start()

        @pl.when((j == 1) & (n + 1 < matrices))
        def _():
            load_a(n + 1, 0).start()
            load_a(n + 1, 1).start()

        @pl.when(t >= 2)
        def _():
            send_term(t - 2).wait_send()

        tsend[s] = _dot(abuf[sa, 0], gbuf[s]).astype(tsend.dtype)
        send_term(t).start()

        @pl.when(j == 0)
        def _():
            load_a(n, 1).wait()

        part = _dot(abuf[sa, 1], gbuf[s])
        send_term(t).wait_recv()
        total = part + term[s].astype(jnp.float32)
        on_first = x == 0
        own[lax.rem(t, KEPT)] = jnp.where(on_first, total[:quarter], total[quarter:])

        @pl.when(t >= SENDS)
        def _():
            send_x(t - SENDS).wait_send()

        xsend[lax.rem(t, SENDS)] = jnp.where(on_first, total[quarter:], total[:quarter]).astype(xsend.dtype)
        send_x(t).start()

        @pl.when(t >= LAG)
        def _():
            finish(t - LAG)

        return 0

    lax.fori_loop(0, tiles, step, 0)

    def rest(u, _):
        finish(u)
        return 0

    lax.fori_loop(tiles - LAG, tiles, rest, 0)

    def drain(t, _):
        send_x(t).wait_send()
        return 0

    lax.fori_loop(tiles - SENDS, tiles, drain, 0)
    for t in (tiles - 2, tiles - 1):
        send_term(t).wait_send()
        wait_f(t)


def reduce_to_quarters(a, g):
    _, matrices, k, d = a.shape
    half, quarter, tiles = d // 2, d // 4, matrices * (g.shape[3] // CT)
    flops = 2 * k * d * g.shape[3] * matrices
    return pl.pallas_call(
        reduce_kernel,
        out_shape=tuple(jax.ShapeDtypeStruct((quarter, c), jnp.bfloat16) for _, _, c in PIECES),
        in_specs=[ANY] * 2,
        out_specs=(ANY,) * len(PIECES),
        scratch_shapes=[
            pltpu.VMEM((2, 2, k, half), jnp.bfloat16),
            pltpu.VMEM((2, k, CT), jnp.bfloat16),
            pltpu.VMEM((2, half, CT), jnp.bfloat16),
            pltpu.VMEM((2, half, CT), jnp.bfloat16),
            pltpu.VMEM((SENDS, quarter, CT), jnp.bfloat16),
            pltpu.VMEM((KEPT, quarter, CT), jnp.float32),
            pltpu.VMEM((tiles, quarter, CT), jnp.bfloat16),
            pltpu.VMEM((2, quarter, CT), jnp.bfloat16),
            pltpu.SemaphoreType.DMA((2, 2)),
            pltpu.SemaphoreType.DMA((2,)),
            pltpu.SemaphoreType.DMA((2,)),
            pltpu.SemaphoreType.DMA((2,)),
            pltpu.SemaphoreType.DMA((SENDS,)),
            pltpu.SemaphoreType.DMA((tiles,)),
            pltpu.SemaphoreType.DMA((2,)),
        ],
        name="reduce",
        compiler_params=pltpu.CompilerParams(vmem_limit_bytes=VMEM, collective_id=0, has_side_effects=True),
        cost_estimate=pl.CostEstimate(flops=flops, bytes_accessed=2 * a.size + 2 * g.size, transcendentals=0),
    )(a, g)


def place(pos, mine, passed, out, dep, shape, n, c0, c, other_chip):
    quarter, ct = mine.shape[0], min(c, 512)
    tiles = c // ct

    def body(pos, mine_ref, passed_ref, dep_ref, *rest):
        o_ref = rest[-1]
        for s, ref in enumerate((mine_ref, passed_ref)):
            @pl.when(pl.program_id(0) == s)
            def _():
                o_ref[0] = ref[...]

    def to(p, j, pos):
        core = jnp.where(p == 0, pos[0], 1 - pos[0])
        return n, 2 * core + (1 - pos[1] if other_chip else pos[1]), c0 // ct + j

    extra = () if out is None else (out,)
    return pl.pallas_call(
        body,
        out_shape=jax.ShapeDtypeStruct(shape, jnp.bfloat16),
        grid_spec=pltpu.PrefetchScalarGridSpec(
            num_scalar_prefetch=1,
            grid=(2, tiles),
            in_specs=[
                pl.BlockSpec((quarter, ct), lambda p, j, pos: (0, jnp.where(p == 0, j, tiles - 1))),
                pl.BlockSpec((quarter, ct), lambda p, j, pos: (0, jnp.where(p == 1, j, 0))),
            ]
            + [ANY] * (1 + len(extra)),
            out_specs=pl.BlockSpec((1, quarter, ct), to),
        ),
        input_output_aliases={4: 0} if extra else {},
        compiler_params=pltpu.CompilerParams(vmem_limit_bytes=VMEM),
        cost_estimate=pl.CostEstimate(flops=quarter * c * 400, bytes_accessed=quarter * c * 8, transcendentals=0),
    )(pos, mine, passed, dep, *extra)


def solution(mesh):
    over_x = [(0, 2), (2, 0), (1, 3), (3, 1)]
    over_core = [(0, 1), (1, 0), (2, 3), (3, 2)]

    def swap(t, pairs):
        return lax.ppermute(t, "dp", pairs)

    def body(a, g):
        me = lax.axis_index("dp")
        pos = jnp.stack([lax.rem(me, 2), lax.div(me, 2)]).astype(jnp.int32)
        _, matrices, _, d = a.shape
        shape = (matrices, d, g.shape[3])
        f = reduce_to_quarters(a, g)
        z = [swap(t, over_x) for t in f]
        cf = [swap(t, over_core) for t in f]
        out = None
        for i, piece in enumerate(PIECES):
            out = place(pos, f[i], cf[i], out, pos, shape, *piece, False)
        for i, piece in enumerate(PIECES):
            cz = swap(z[i], over_core)
            out = place(pos, z[i], cz, out, pos, shape, *piece, True)
        return out

    spec = P(("rep", "dp"))
    return jax.shard_map(body, mesh=mesh, in_specs=(spec, spec), out_specs=P("rep"), check_vma=False)
```

time: 1680 us -> 841 us (0.50)
  blocking collectives: 1480 us -> 0 us
  Pallas kernels: 0 us -> 583 us
  waiting for transfers between devices: 0 us -> 244 us
  matrix products: 199 us -> 0 us
    dot_general x1 -> x0, blocking collectives: 1480 us -> none  [step(): jnp.einsum('rsntd,rsntf->rndf', a, g, preferred_element_type=jnp.float32)]
    pallas_call x0 -> x17, Pallas kernels: none -> 583 us  [the longest x1 483 us: reduce_to_quarters(): pl.pallas_call(reduce_kernel, out_shape=tuple((jax.ShapeDtypeStruct((quar...]
    ppermute x0 -> x24, waiting for transfers between devices: none -> 244 us  [swap(): return lax.ppermute(t, 'dp', pairs)]
    dot_general x1 -> x0, matrix products: 199 us -> none  [step(): jnp.einsum('rsntd,rsntf->rndf', a, g, preferred_element_type=jnp.float32)]
  transfers between devices with their start and end apart: 0 -> 24, of which waited for: 0 -> 7; matrix products, arithmetic and copies ran while one was open for 0% -> 0% of each run, Pallas kernels for 0% -> 12%
where the time goes in v2:
time: 841 us; the launch traced here: 839 us
  Pallas kernels  583 us (69%)
  waiting for transfers between devices  244 us (29%)
  starting transfers between devices  9.34 us (1%)
    pallas_call x1, Pallas kernels, reduce_to_quarters(): pl.pallas_call(reduce_kernel, out_shape=tuple((jax.ShapeDtypeStruct((quar...  483 us
    ppermute x24, waiting for transfers between devices, swap(): return lax.ppermute(t, 'dp', pairs)  244 us
    pallas_call x16, Pallas kernels, place(): pl.pallas_call(body, out_shape=jax.ShapeDtypeStruct(shape, jnp.bfloat16),...  100 us
  transfers between devices with their start and end apart: 24, of which 7 were waited for; matrix products, arithmetic and copies ran while one was open for 0% of the time, Pallas kernels for 12%

profile of v2, /device:TPU:0, one launch (start us, length us, event | category | flops | bytes accessed | tf_op | source)
XLA Modules:
  0.0 839.2 jit_solution(577974340265618427)
XLA Ops:
  0.0 482.7 %reduce.1 = (bf16[384,3584]{1,0:T(8,128)(2,1)}, bf16[384,3584]{1,0:T(8,128)(2,1)}, bf16[384,3584]{1,0:T(8,128)(2,1)}, bf16[384,1536]{1,0:T(8,128)(2,1)}, bf16[38...) custom-call(bf16[1,4,4096,1536]{3,2,1,0:T(8,128)(2,1)} %a.1, ...), custom_call_target="tpu_custom_call" | custom-call | flops 180388626432 | bytes 167772160 | tf_op jit(solution)/shard_map/reduce/pallas_call | solution.py:161
  483.3 2.0 collective-permute-start
  485.6 5.7 collective-permute-done.2.mine_ref
  491.3 4.2 collective-permute-done.mine_ref
  496.2 24.2 %collective-permute-done.4.mine_ref = bf16[384,512]{1,0:T(8,128)(2,1)} collective-permute-done((bf16[384,512]{1,0:T(8,128)(2,1)}, bf16[384,512]{1,0:T(8,128)(2,1)}, u32[]{:S(2)}, u32[]{:S(2)}) %collective-permute-start.4) | collective-permute-done | bytes 393248 | tf_op jit(solution)/shard_map/ppermute | solution.py:229
  524.5 200.7 %collective-permute-done.8.mine_ref = bf16[384,1536]{1,0:T(8,128)(2,1)} collective-permute-done((bf16[384,1536]{1,0:T(8,128)(2,1)}, bf16[384,1536]{1,0:T(8,128)(2,1)}, u32[]{:S(2)}, u32[]{:S(2)}) %collective-permute-start.8) | collective-permute-done | bytes 1179680 | tf_op jit(solution)/shard_map/ppermute | solution.py:229
  730.7 3.8 collective-permute-done.21.passed_ref
  735.3 3.2 collective-permute-done.15.passed_ref
  738.6 10.7 %shard_map.28.rest_0_ = bf16[4,1536,3584]{2,1,0:T(8,128)(2,1)} custom-call(s32[2]{0:T(128)} %pad_add_fusion.pos.dep_ref, bf16[384,3584]{1,0:T(8,128)(2,1)} %get-tuple-element.20.mine_ref, bf16[384,3584]{1,0:T(8,128)(2,1)} %copy-done.1, s32[2]{0:T(128)} %pad_add_fusion.pos.dep_ref), custom_call_target="tpu_custom_call" | custom-call | flops 550502400 | bytes 11010048 | tf_op jit(solution)/shard_map/pallas_call | solution.py:205
  749.3 10.7 %shard_map.29.rest_0_ = bf16[4,1536,3584]{2,1,0:T(8,128)(2,1)} custom-call(s32[2]{0:T(128)} %pad_add_fusion.pos.dep_ref, bf16[384,3584]{1,0:T(8,128)(2,1)} %get-tuple-element.19.mine_ref, bf16[384,3584]{1,0:T(8,128)(2,1)} %collective-permute-done.22.passed_ref, s32[2]{0:T(128)} %pad_add_fusion.pos.dep_ref, ...), custom_call_target="tpu_custom_call", output_to_operand_aliasing={{}: (4, {})} | custom-call | flops 550502400 | bytes 11010048 | tf_op jit(solution)/shard_map/pallas_call | solution.py:205
  760.1 10.7 %shard_map.30.rest_0_ = bf16[4,1536,3584]{2,1,0:T(8,128)(2,1)} custom-call(s32[2]{0:T(128)} %pad_add_fusion.pos.dep_ref, bf16[384,3584]{1,0:T(8,128)(2,1)} %get-tuple-element.18.mine_ref, bf16[384,3584]{1,0:T(8,128)(2,1)} %collective-permute-done.21.passed_ref, s32[2]{0:T(128)} %pad_add_fusion.pos.dep_ref, ...), custom_call_target="tpu_custom_call", output_to_operand_aliasing={{}: (4, {})} | custom-call | flops 550502400 | bytes 11010048 | tf_op jit(solution)/shard_map/pallas_call | solution.py:205
  770.8 5.7 shard_map.31.rest_0_
  776.5 4.5 shard_map.32.rest_0_
  781.0 2.7 shard_map.33.rest_0_
  783.7 2.5 shard_map.34.rest_0_
  786.2 2.5 shard_map.35.rest_0_
  789.2 10.7 %shard_map.36.rest_0_ = bf16[4,1536,3584]{2,1,0:T(8,128)(2,1)} custom-call(s32[2]{0:T(128)} %pad_add_fusion.pos.dep_ref, bf16[384,3584]{1,0:T(8,128)(2,1)} %copy-done, bf16[384,3584]{1,0:T(8,128)(2,1)} %collective-permute-done.15.passed_ref, s32[2]{0:T(128)} %pad_add_fusion.pos.dep_ref, ...), custom_call_target="tpu_custom_call", output_to_operand_aliasing={{}: (4, {})} | custom-call | flops 550502400 | bytes 11010048 | tf_op jit(solution)/shard_map/pallas_call | solution.py:205
  799.9 10.7 %shard_map.37.rest_0_ = bf16[4,1536,3584]{2,1,0:T(8,128)(2,1)} custom-call(s32[2]{0:T(128)} %pad_add_fusion.pos.dep_ref, bf16[384,3584]{1,0:T(8,128)(2,1)} %collective-permute-done.12.mine_ref, bf16[384,3584]{1,0:T(8,128)(2,1)} %collective-permute-done.13.passed_ref, s32[2]{0:T(128)} %pad_add_fusion.pos.dep_ref, ...), custom_call_target="tpu_custom_call", output_to_operand_aliasing={{}: (4, {})} | custom-call | flops 550502400 | bytes 11010048 | tf_op jit(solution)/shard_map/pallas_call | solution.py:205
  810.6 10.7 %shard_map.38.rest_0_ = bf16[4,1536,3584]{2,1,0:T(8,128)(2,1)} custom-call(s32[2]{0:T(128)} %pad_add_fusion.pos.dep_ref, bf16[384,3584]{1,0:T(8,128)(2,1)} %collective-permute-done.10.mine_ref, bf16[384,3584]{1,0:T(8,128)(2,1)} %collective-permute-done.11.passed_ref, s32[2]{0:T(128)} %pad_add_fusion.pos.dep_ref, ...), custom_call_target="tpu_custom_call", output_to_operand_aliasing={{}: (4, {})} | custom-call | flops 550502400 | bytes 11010048 | tf_op jit(solution)/shard_map/pallas_call | solution.py:205
  821.3 5.7 shard_map.39.rest_0_
  827.1 4.5 shard_map.40.rest_0_
  831.6 2.7 shard_map.41.rest_0_
  834.3 2.5 shard_map.42.rest_0_
  836.8 2.5 shard_map.43
  (60 shorter events, 12.5 us)
Async XLA Ops:
  482.7 13.5 %collective-permute-start.18 = (bf16[384,512]{1,0:T(8,128)(2,1)}, bf16[384,512]{1,0:T(8,128)(2,1)S(1)}, u32[]{:S(2)}, u32[]{:S(2)}) collective-permute-start(bf16[384,512]{1,0:T(8,128)(2,1)} %get-tuple-element.15.mine_ref), channel_id=1, source_target_pairs={{0,1},{1,0},{2,3},{3,2},{4,5},{5,4},{6,7},{7,6}} | collective-permute-start | bytes 1179656 | tf_op jit(solution)/shard_map/ppermute | solution.py:229
  482.8 2.6 collective-permute-start.17
  483.3 2.1 collective-permute-start.16
  483.3 8.0 collective-permute-start.2
  483.3 12.2 %collective-permute-start = (bf16[384,256]{1,0:T(8,128)(2,1)}, bf16[384,256]{1,0:T(8,128)(2,1)S(1)}, u32[]{:S(2)}, u32[]{:S(2)}) collective-permute-start(bf16[384,256]{1,0:T(8,128)(2,1)} %get-tuple-element.13.mine_ref), channel_id=1, source_target_pairs={{0,2},{2,0},{1,3},{3,1},{4,6},{6,4},{5,7},{7,5}} | collective-permute-start | bytes 589832 | tf_op jit(solution)/shard_map/ppermute | solution.py:229
  485.3 35.3 %collective-permute-start.19 = (bf16[384,1024]{1,0:T(8,128)(2,1)}, bf16[384,1024]{1,0:T(8,128)(2,1)S(1)}, u32[]{:S(2)}, u32[]{:S(2)}) collective-permute-start(bf16[384,1024]{1,0:T(8,128)(2,1)} %get-tuple-element.16.mine_ref), channel_id=1, source_target_pairs={{0,1},{1,0},{2,3},{3,2},{4,5},{5,4},{6,7},{7,6}} | collective-permute-start | bytes 2359304 | tf_op jit(solution)/shard_map/ppermute | solution.py:229
  485.4 37.1 %collective-permute-start.6 = (bf16[384,1024]{1,0:T(8,128)(2,1)}, bf16[384,1024]{1,0:T(8,128)(2,1)}, u32[]{:S(2)}, u32[]{:S(2)}) collective-permute-start(bf16[384,1024]{1,0:T(8,128)(2,1)} %get-tuple-element.16.mine_ref), channel_id=1, source_target_pairs={{0,2},{2,0},{1,3},{3,1},{4,6},{6,4},{5,7},{7,5}} | collective-permute-start | bytes 2359304 | tf_op jit(solution)/shard_map/ppermute | solution.py:229
  491.3 31.4 %collective-permute-start.20 = (bf16[384,1536]{1,0:T(8,128)(2,1)}, bf16[384,1536]{1,0:T(8,128)(2,1)S(1)}, u32[]{:S(2)}, u32[]{:S(2)}) collective-permute-start(bf16[384,1536]{1,0:T(8,128)(2,1)} %get-tuple-element.17.mine_ref), channel_id=1, source_target_pairs={{0,1},{1,0},{2,3},{3,2},{4,5},{5,4},{6,7},{7,6}} | collective-permute-start | bytes 3538952 | tf_op jit(solution)/shard_map/ppermute | solution.py:229
  496.2 229.0 %collective-permute-start.23 = (bf16[384,3584]{1,0:T(8,128)(2,1)}, bf16[384,3584]{1,0:T(8,128)(2,1)S(1)}, u32[]{:S(2)}, u32[]{:S(2)}) collective-permute-start(bf16[384,3584]{1,0:T(8,128)(2,1)} %get-tuple-element.20.mine_ref), channel_id=1, source_target_pairs={{0,1},{1,0},{2,3},{3,2},{4,5},{5,4},{6,7},{7,6}} | collective-permute-start | bytes 8257544 | tf_op jit(solution)/shard_map/ppermute | solution.py:229
  496.2 24.2 %collective-permute-start.4 = (bf16[384,512]{1,0:T(8,128)(2,1)}, bf16[384,512]{1,0:T(8,128)(2,1)}, u32[]{:S(2)}, u32[]{:S(2)}) collective-permute-start(bf16[384,512]{1,0:T(8,128)(2,1)} %get-tuple-element.15.mine_ref), channel_id=1, source_target_pairs={{0,2},{2,0},{1,3},{3,1},{4,6},{6,4},{5,7},{7,5}} | collective-permute-start | bytes 1179656 | tf_op jit(solution)/shard_map/ppermute | solution.py:229
  520.4 205.3 %collective-permute-start.14 = (bf16[384,3584]{1,0:T(8,128)(2,1)}, bf16[384,3584]{1,0:T(8,128)(2,1)S(1)}, u32[]{:S(2)}, u32[]{:S(2)}) collective-permute-start(bf16[384,3584]{1,0:T(8,128)(2,1)} %get-tuple-element.20.mine_ref), channel_id=1, source_target_pairs={{0,2},{2,0},{1,3},{3,1},{4,6},{6,4},{5,7},{7,5}} | collective-permute-start | bytes 8257544 | tf_op jit(solution)/shard_map/ppermute | solution.py:229
  520.7 207.5 %collective-permute-start.12 = (bf16[384,3584]{1,0:T(8,128)(2,1)}, bf16[384,3584]{1,0:T(8,128)(2,1)}, u32[]{:S(2)}, u32[]{:S(2)}) collective-permute-start(bf16[384,3584]{1,0:T(8,128)(2,1)} %get-tuple-element.19.mine_ref), channel_id=1, source_target_pairs={{0,2},{2,0},{1,3},{3,1},{4,6},{6,4},{5,7},{7,5}} | collective-permute-start | bytes 8257544 | tf_op jit(solution)/shard_map/ppermute | solution.py:229
  522.4 205.8 %collective-permute-start.10 = (bf16[384,3584]{1,0:T(8,128)(2,1)}, bf16[384,3584]{1,0:T(8,128)(2,1)}, u32[]{:S(2)}, u32[]{:S(2)}) collective-permute-start(bf16[384,3584]{1,0:T(8,128)(2,1)} %get-tuple-element.18.mine_ref), channel_id=1, source_target_pairs={{0,2},{2,0},{1,3},{3,1},{4,6},{6,4},{5,7},{7,5}} | collective-permute-start | bytes 8257544 | tf_op jit(solution)/shard_map/ppermute | solution.py:229
  522.7 202.4 %collective-permute-start.8 = (bf16[384,1536]{1,0:T(8,128)(2,1)}, bf16[384,1536]{1,0:T(8,128)(2,1)}, u32[]{:S(2)}, u32[]{:S(2)}) collective-permute-start(bf16[384,1536]{1,0:T(8,128)(2,1)} %get-tuple-element.17.mine_ref), channel_id=1, source_target_pairs={{0,2},{2,0},{1,3},{3,1},{4,6},{6,4},{5,7},{7,5}} | collective-permute-start | bytes 3538952 | tf_op jit(solution)/shard_map/ppermute | solution.py:229
  725.2 5.4 collective-permute-start.22
  725.2 9.4 %collective-permute-start.21 = (bf16[384,3584]{1,0:T(8,128)(2,1)}, bf16[384,3584]{1,0:T(8,128)(2,1)}, u32[]{:S(2)}, u32[]{:S(2)}) collective-permute-start(bf16[384,3584]{1,0:T(8,128)(2,1)} %get-tuple-element.18.mine_ref), channel_id=1, source_target_pairs={{0,1},{1,0},{2,3},{3,2},{4,5},{5,4},{6,7},{7,6}} | collective-permute-start | bytes 8257544 | tf_op jit(solution)/shard_map/ppermute | solution.py:229
  727.7 10.8 %collective-permute-start.15 = (bf16[384,3584]{1,0:T(8,128)(2,1)S(1)}, bf16[384,3584]{1,0:T(8,128)(2,1)}, u32[]{:S(2)}, u32[]{:S(2)}) collective-permute-start(bf16[384,3584]{1,0:T(8,128)(2,1)S(1)} %collective-permute-done.14.mine_ref), channel_id=1, source_target_pairs={{0,1},{1,0},{2,3},{3,2},{4,5},{5,4},{6,7},{7,6}} | collective-permute-start | bytes 8257544 | tf_op jit(solution)/shard_map/ppermute | solution.py:229
  728.2 60.5 %collective-permute-start.13 = (bf16[384,3584]{1,0:T(8,128)(2,1)}, bf16[384,3584]{1,0:T(8,128)(2,1)}, u32[]{:S(2)}, u32[]{:S(2)}) collective-permute-start(bf16[384,3584]{1,0:T(8,128)(2,1)} %collective-permute-done.12.mine_ref), channel_id=1, source_target_pairs={{0,1},{1,0},{2,3},{3,2},{4,5},{5,4},{6,7},{7,6}} | collective-permute-start | bytes 8257544 | tf_op jit(solution)/shard_map/ppermute | solution.py:229
  728.3 60.8 %collective-permute-start.11 = (bf16[384,3584]{1,0:T(8,128)(2,1)}, bf16[384,3584]{1,0:T(8,128)(2,1)}, u32[]{:S(2)}, u32[]{:S(2)}) collective-permute-start(bf16[384,3584]{1,0:T(8,128)(2,1)} %collective-permute-done.10.mine_ref), channel_id=1, source_target_pairs={{0,1},{1,0},{2,3},{3,2},{4,5},{5,4},{6,7},{7,6}} | collective-permute-start | bytes 8257544 | tf_op jit(solution)/shard_map/ppermute | solution.py:229
  730.6 90.8 %collective-permute-start.9 = (bf16[384,1536]{1,0:T(8,128)(2,1)}, bf16[384,1536]{1,0:T(8,128)(2,1)}, u32[]{:S(2)}, u32[]{:S(2)}) collective-permute-start(bf16[384,1536]{1,0:T(8,128)(2,1)} %collective-permute-done.8.mine_ref), channel_id=1, source_target_pairs={{0,1},{1,0},{2,3},{3,2},{4,5},{5,4},{6,7},{7,6}} | collective-permute-start | bytes 3538952 | tf_op jit(solution)/shard_map/ppermute | solution.py:229
  734.5 92.6 %collective-permute-start.7 = (bf16[384,1024]{1,0:T(8,128)(2,1)}, bf16[384,1024]{1,0:T(8,128)(2,1)}, u32[]{:S(2)}, u32[]{:S(2)}) collective-permute-start(bf16[384,1024]{1,0:T(8,128)(2,1)} %collective-permute-done.6.mine_ref), channel_id=1, source_target_pairs={{0,1},{1,0},{2,3},{3,2},{4,5},{5,4},{6,7},{7,6}} | collective-permute-start | bytes 2359304 | tf_op jit(solution)/shard_map/ppermute | solution.py:229
  738.5 93.1 %collective-permute-start.5 = (bf16[384,512]{1,0:T(8,128)(2,1)}, bf16[384,512]{1,0:T(8,128)(2,1)}, u32[]{:S(2)}, u32[]{:S(2)}) collective-permute-start(bf16[384,512]{1,0:T(8,128)(2,1)} %collective-permute-done.4.mine_ref), channel_id=1, source_target_pairs={{0,1},{1,0},{2,3},{3,2},{4,5},{5,4},{6,7},{7,6}} | collective-permute-start | bytes 1179656 | tf_op jit(solution)/shard_map/ppermute | solution.py:229
  788.6 45.6 %collective-permute-start.3 = (bf16[384,256]{1,0:T(8,128)(2,1)}, bf16[384,256]{1,0:T(8,128)(2,1)}, u32[]{:S(2)}, u32[]{:S(2)}) collective-permute-start(bf16[384,256]{1,0:T(8,128)(2,1)} %copy-done.6), channel_id=1, source_target_pairs={{0,1},{1,0},{2,3},{3,2},{4,5},{5,4},{6,7},{7,6}} | collective-permute-start | bytes 589832 | tf_op jit(solution)/shard_map/ppermute | solution.py:229
  789.0 47.7 %collective-permute-start.1 = (bf16[384,256]{1,0:T(8,128)(2,1)}, bf16[384,256]{1,0:T(8,128)(2,1)}, u32[]{:S(2)}, u32[]{:S(2)}) collective-permute-start(bf16[384,256]{1,0:T(8,128)(2,1)} %copy-done.5), channel_id=1, source_target_pairs={{0,1},{1,0},{2,3},{3,2},{4,5},{5,4},{6,7},{7,6}} | collective-permute-start | bytes 589832 | tf_op jit(solution)/shard_map/ppermute | solution.py:229
  (9 other events, 675.3 us)

commit v3 on v2

--- a/solution.py
+++ b/solution.py
@@ -6,11 +6,11 @@
 from jax.sharding import PartitionSpec as P
 
 
-CT = 256
-SENDS = 8
-KEPT = 16
-LAG = 8
-PIECES = ((0, 0, 3584), (1, 0, 3584), (2, 0, 3584), (3, 0, 1536), (3, 1536, 1024), (3, 2560, 512), (3, 3072, 256), (3, 3328, 256))
+CT = 512
+SENDS = 4
+KEPT = 6
+LAG = 5
+PIECES = ((0, 0, 3584), (1, 0, 3584), (2, 0, 3584), (3, 0, 1536), (3, 1536, 1024), (3, 2560, 512), (3, 3072, 512))
 VMEM = 67043328
 ANY = pl.BlockSpec(memory_space=pl.ANY)
 MESH = pl.DeviceIdType.MESH
@@ -22,7 +22,7 @@
 
 def reduce_kernel(a, g, *refs):
     outs, scratch = refs[: len(PIECES)], refs[len(PIECES) :]
-    abuf, gbuf, tsend, term, xsend, own, got, fbuf, a_sem, g_sem, ts_sem, tr_sem, xs_sem, xr_sem, f_sem = scratch
+    abuf, gbuf, tsend, term, pend, xsend, own, got, fbuf, a_sem, g_sem, ts_sem, tr_sem, xs_sem, xr_sem, f_sem = scratch
     _, matrices, _, d = a.shape
     half, quarter, per = d // 2, d // 4, g.shape[3] // CT
     tiles = matrices * per
@@ -76,6 +76,19 @@
             def _():
                 store_f(u, out, c0).start()
 
+    def own_sum(t):
+        send_term(t).wait_recv()
+
+        @pl.when(t >= SENDS)
+        def _():
+            send_x(t - SENDS).wait_send()
+
+        rows = [pl.ds(pl.multiple_of(quarter * q, quarter), quarter) for q in (x, 1 - x)]
+        s = lax.rem(t, 2)
+        own[lax.rem(t, KEPT)] = pend[rows[0], :] + term[s, rows[0], :].astype(jnp.float32)
+        xsend[lax.rem(t, SENDS)] = (pend[rows[1], :] + term[s, rows[1], :].astype(jnp.float32)).astype(xsend.dtype)
+        send_x(t).start()
+
     load_a(0, 0).start()
     load_g(0).start()
     barrier = pltpu.get_barrier_semaphore()
@@ -111,24 +124,22 @@
             send_term(t - 2).wait_send()
 
         tsend[s] = _dot(abuf[sa, 0], gbuf[s]).astype(tsend.dtype)
+
+        @pl.when(t >= 2)
+        def _():
+            own_sum(t - 1)
+
         send_term(t).start()
 
         @pl.when(j == 0)
         def _():
             load_a(n, 1).wait()
 
-        part = _dot(abuf[sa, 1], gbuf[s])
-        send_term(t).wait_recv()
-        total = part + term[s].astype(jnp.float32)
-        on_first = x == 0
-        own[lax.rem(t, KEPT)] = jnp.where(on_first, total[:quarter], total[quarter:])
-
-        @pl.when(t >= SENDS)
-        def _():
-            send_x(t - SENDS).wait_send()
-
-        xsend[lax.rem(t, SENDS)] = jnp.where(on_first, total[quarter:], total[:quarter]).astype(xsend.dtype)
-        send_x(t).start()
+        pend[...] = _dot(abuf[sa, 1], gbuf[s])
+
+        @pl.when(t == 0)
+        def _():
+            own_sum(0)
 
         @pl.when(t >= LAG)
         def _():
@@ -137,6 +148,7 @@
         return 0
 
     lax.fori_loop(0, tiles, step, 0)
+    own_sum(tiles - 1)
 
     def rest(u, _):
         finish(u)
@@ -168,6 +180,7 @@
             pltpu.VMEM((2, k, CT), jnp.bfloat16),
             pltpu.VMEM((2, half, CT), jnp.bfloat16),
             pltpu.VMEM((2, half, CT), jnp.bfloat16),
+            pltpu.VMEM((half, CT), jnp.float32),
             pltpu.VMEM((SENDS, quarter, CT), jnp.bfloat16),
             pltpu.VMEM((KEPT, quarter, CT), jnp.float32),
             pltpu.VMEM((tiles, quarter, CT), jnp.bfloat16),

time: 841 us -> 611 us (0.73)
  Pallas kernels: 583 us -> 350 us
    pallas_call x1, Pallas kernels: 483 us -> 254 us  [reduce_to_quarters(): pl.pallas_call(reduce_kernel, out_shape=tuple((jax.ShapeDtypeStruct((quar...]
    pallas_call x16 -> x14, Pallas kernels: 100 us -> 95.6 us  [place(): pl.pallas_call(body, out_shape=jax.ShapeDtypeStruct(shape, jnp.bfloat16),...]
    ppermute x24 -> x21, waiting for transfers between devices: 244 us -> 246 us  [swap(): return lax.ppermute(t, 'dp', pairs)]
  transfers between devices with their start and end apart: 24 -> 21, of which waited for: 7 -> 7; matrix products, arithmetic and copies ran while one was open for 0% -> 0% of each run, Pallas kernels for 12% -> 15%
where the time goes in v3:
time: 611 us; the launch traced here: 609 us
  Pallas kernels  350 us (57%)
  waiting for transfers between devices  246 us (40%)
  starting transfers between devices  9.14 us (1%)
    pallas_call x1, Pallas kernels, reduce_to_quarters(): pl.pallas_call(reduce_kernel, out_shape=tuple((jax.ShapeDtypeStruct((quar...  254 us
    ppermute x21, waiting for transfers between devices, swap(): return lax.ppermute(t, 'dp', pairs)  246 us
    pallas_call x14, Pallas kernels, place(): pl.pallas_call(body, out_shape=jax.ShapeDtypeStruct(shape, jnp.bfloat16),...  95.6 us
  transfers between devices with their start and end apart: 21, of which 7 were waited for; matrix products, arithmetic and copies ran while one was open for 0% of the time, Pallas kernels for 15%

profile of v3, /device:TPU:0, one launch (start us, length us, event | category | flops | bytes accessed | tf_op | source)
XLA Modules:
  0.0 608.8 jit_solution(2505137770685356215)
XLA Ops:
  0.0 254.3 %reduce.1 = (bf16[384,3584]{1,0:T(8,128)(2,1)}, bf16[384,3584]{1,0:T(8,128)(2,1)}, bf16[384,3584]{1,0:T(8,128)(2,1)}, bf16[384,1536]{1,0:T(8,128)(2,1)}, bf16[38...) custom-call(bf16[1,4,4096,1536]{3,2,1,0:T(8,128)(2,1)} %a.1, bf16[1,4,4096,3584]{3,2,1,0:T(8,128)(2,1)} %g.1), custom_call_target="tpu_custom_call" | custom-call | flops 180388626432 | bytes 167772160 | tf_op jit(solution)/shard_map/reduce/pallas_call | solution.py:173
  254.9 2.0 collective-permute-start.4
  258.6 8.5 %collective-permute-done.2.mine_ref = bf16[384,512]{1,0:T(8,128)(2,1)} collective-permute-done((bf16[384,512]{1,0:T(8,128)(2,1)}, bf16[384,512]{1,0:T(8,128)(2,1)}, u32[]{:S(2)}, u32[]{:S(2)}) %collective-permute-start.2) | collective-permute-done | bytes 393248 | tf_op jit(solution)/shard_map/ppermute | solution.py:242
  267.1 24.3 %collective-permute-done.mine_ref = bf16[384,512]{1,0:T(8,128)(2,1)} collective-permute-done((bf16[384,512]{1,0:T(8,128)(2,1)}, bf16[384,512]{1,0:T(8,128)(2,1)}, u32[]{:S(2)}, u32[]{:S(2)}) %collective-permute-start) | collective-permute-done | bytes 393248 | tf_op jit(solution)/shard_map/ppermute | solution.py:242
  295.5 200.3 %collective-permute-done.6.mine_ref = bf16[384,1536]{1,0:T(8,128)(2,1)} collective-permute-done((bf16[384,1536]{1,0:T(8,128)(2,1)}, bf16[384,1536]{1,0:T(8,128)(2,1)}, u32[]{:S(2)}, u32[]{:S(2)}) %collective-permute-start.6) | collective-permute-done | bytes 1179680 | tf_op jit(solution)/shard_map/ppermute | solution.py:242
  496.3 2.0 copy-done
  499.4 1.9 collective-permute-done.19.passed_ref
  501.4 3.8 collective-permute-done.18.passed_ref
  505.9 3.2 collective-permute-done.13.passed_ref
  509.2 3.8 collective-permute-done.11.passed_ref
  513.2 10.7 %shard_map.28.rest_0_ = bf16[4,1536,3584]{2,1,0:T(8,128)(2,1)} custom-call(s32[2]{0:T(128)} %pad_add_fusion.pos.dep_ref, bf16[384,3584]{1,0:T(8,128)(2,1)} %get-tuple-element.18.mine_ref, bf16[384,3584]{1,0:T(8,128)(2,1)} %copy-done.1, s32[2]{0:T(128)} %pad_add_fusion.pos.dep_ref), custom_call_target="tpu_custom_call" | custom-call | flops 550502400 | bytes 11010048 | tf_op jit(solution)/shard_map/pallas_call | solution.py:218
  523.9 10.7 %shard_map.29.rest_0_ = bf16[4,1536,3584]{2,1,0:T(8,128)(2,1)} custom-call(s32[2]{0:T(128)} %pad_add_fusion.pos.dep_ref, bf16[384,3584]{1,0:T(8,128)(2,1)} %get-tuple-element.17.mine_ref, bf16[384,3584]{1,0:T(8,128)(2,1)} %collective-permute-done.19.passed_ref, s32[2]{0:T(128)} %pad_add_fusion.pos.dep_ref, ...), custom_call_target="tpu_custom_call", output_to_operand_aliasing={{}: (4, {})} | custom-call | flops 550502400 | bytes 11010048 | tf_op jit(solution)/shard_map/pallas_call | solution.py:218
  534.6 10.7 %shard_map.30.rest_0_ = bf16[4,1536,3584]{2,1,0:T(8,128)(2,1)} custom-call(s32[2]{0:T(128)} %pad_add_fusion.pos.dep_ref, bf16[384,3584]{1,0:T(8,128)(2,1)} %get-tuple-element.16.mine_ref, bf16[384,3584]{1,0:T(8,128)(2,1)} %collective-permute-done.18.passed_ref, s32[2]{0:T(128)} %pad_add_fusion.pos.dep_ref, ...), custom_call_target="tpu_custom_call", output_to_operand_aliasing={{}: (4, {})} | custom-call | flops 550502400 | bytes 11010048 | tf_op jit(solution)/shard_map/pallas_call | solution.py:218
  545.4 5.7 shard_map.31.rest_0_
  551.1 4.5 shard_map.32.rest_0_
  555.6 2.7 shard_map.33.rest_0_
  558.3 2.7 shard_map.34.rest_0_
  561.0 10.7 %shard_map.35.rest_0_ = bf16[4,1536,3584]{2,1,0:T(8,128)(2,1)} custom-call(s32[2]{0:T(128)} %pad_add_fusion.pos.dep_ref, bf16[384,3584]{1,0:T(8,128)(2,1)} %copy-done, bf16[384,3584]{1,0:T(8,128)(2,1)} %collective-permute-done.13.passed_ref, s32[2]{0:T(128)} %pad_add_fusion.pos.dep_ref, ...), custom_call_target="tpu_custom_call", output_to_operand_aliasing={{}: (4, {})} | custom-call | flops 550502400 | bytes 11010048 | tf_op jit(solution)/shard_map/pallas_call | solution.py:218
  571.7 10.7 %shard_map.36.rest_0_ = bf16[4,1536,3584]{2,1,0:T(8,128)(2,1)} custom-call(s32[2]{0:T(128)} %pad_add_fusion.pos.dep_ref, bf16[384,3584]{1,0:T(8,128)(2,1)} %collective-permute-done.10.mine_ref, bf16[384,3584]{1,0:T(8,128)(2,1)} %collective-permute-done.11.passed_ref, s32[2]{0:T(128)} %pad_add_fusion.pos.dep_ref, ...), custom_call_target="tpu_custom_call", output_to_operand_aliasing={{}: (4, {})} | custom-call | flops 550502400 | bytes 11010048 | tf_op jit(solution)/shard_map/pallas_call | solution.py:218
  582.5 10.7 %shard_map.37.rest_0_ = bf16[4,1536,3584]{2,1,0:T(8,128)(2,1)} custom-call(s32[2]{0:T(128)} %pad_add_fusion.pos.dep_ref, bf16[384,3584]{1,0:T(8,128)(2,1)} %collective-permute-done.8.mine_ref, bf16[384,3584]{1,0:T(8,128)(2,1)} %collective-permute-done.9.passed_ref, s32[2]{0:T(128)} %pad_add_fusion.pos.dep_ref, ...), custom_call_target="tpu_custom_call", output_to_operand_aliasing={{}: (4, {})} | custom-call | flops 550502400 | bytes 11010048 | tf_op jit(solution)/shard_map/pallas_call | solution.py:218
  593.2 5.7 shard_map.38.rest_0_
  598.9 4.5 shard_map.39.rest_0_
  603.4 2.7 shard_map.40.rest_0_
  606.1 2.7 shard_map.41
  (46 shorter events, 9.1 us)
Async XLA Ops:
  254.3 2.6 collective-permute-start.15
  254.3 2.8 collective-permute-start.14
  254.8 12.3 %collective-permute-start.2 = (bf16[384,512]{1,0:T(8,128)(2,1)}, bf16[384,512]{1,0:T(8,128)(2,1)}, u32[]{:S(2)}, u32[]{:S(2)}) collective-permute-start(bf16[384,512]{1,0:T(8,128)(2,1)} %get-tuple-element.13.mine_ref), channel_id=1, source_target_pairs={{0,2},{2,0},{1,3},{3,1},{4,6},{6,4},{5,7},{7,5}} | collective-permute-start | bytes 1179656 | tf_op jit(solution)/shard_map/ppermute | solution.py:242
  254.8 36.9 %collective-permute-start.16 = (bf16[384,1024]{1,0:T(8,128)(2,1)}, bf16[384,1024]{1,0:T(8,128)(2,1)S(1)}, u32[]{:S(2)}, u32[]{:S(2)}) collective-permute-start(bf16[384,1024]{1,0:T(8,128)(2,1)} %get-tuple-element.14.mine_ref), channel_id=1, source_target_pairs={{0,1},{1,0},{2,3},{3,2},{4,5},{5,4},{6,7},{7,6}} | collective-permute-start | bytes 2359304 | tf_op jit(solution)/shard_map/ppermute | solution.py:242
  254.9 38.6 %collective-permute-start.4 = (bf16[384,1024]{1,0:T(8,128)(2,1)}, bf16[384,1024]{1,0:T(8,128)(2,1)}, u32[]{:S(2)}, u32[]{:S(2)}) collective-permute-start(bf16[384,1024]{1,0:T(8,128)(2,1)} %get-tuple-element.14.mine_ref), channel_id=1, source_target_pairs={{0,2},{2,0},{1,3},{3,1},{4,6},{6,4},{5,7},{7,5}} | collective-permute-start | bytes 2359304 | tf_op jit(solution)/shard_map/ppermute | solution.py:242
  256.8 36.9 %collective-permute-start.17 = (bf16[384,1536]{1,0:T(8,128)(2,1)}, bf16[384,1536]{1,0:T(8,128)(2,1)S(1)}, u32[]{:S(2)}, u32[]{:S(2)}) collective-permute-start(bf16[384,1536]{1,0:T(8,128)(2,1)} %get-tuple-element.15.mine_ref), channel_id=1, source_target_pairs={{0,1},{1,0},{2,3},{3,2},{4,5},{5,4},{6,7},{7,6}} | collective-permute-start | bytes 3538952 | tf_op jit(solution)/shard_map/ppermute | solution.py:242
  258.4 237.4 %collective-permute-start.20 = (bf16[384,3584]{1,0:T(8,128)(2,1)}, bf16[384,3584]{1,0:T(8,128)(2,1)S(1)}, u32[]{:S(2)}, u32[]{:S(2)}) collective-permute-start(bf16[384,3584]{1,0:T(8,128)(2,1)} %get-tuple-element.18.mine_ref), channel_id=1, source_target_pairs={{0,1},{1,0},{2,3},{3,2},{4,5},{5,4},{6,7},{7,6}} | collective-permute-start | bytes 8257544 | tf_op jit(solution)/shard_map/ppermute | solution.py:242
  267.1 24.3 %collective-permute-start = (bf16[384,512]{1,0:T(8,128)(2,1)}, bf16[384,512]{1,0:T(8,128)(2,1)}, u32[]{:S(2)}, u32[]{:S(2)}) collective-permute-start(bf16[384,512]{1,0:T(8,128)(2,1)} %get-tuple-element.12.mine_ref), channel_id=1, source_target_pairs={{0,2},{2,0},{1,3},{3,1},{4,6},{6,4},{5,7},{7,5}} | collective-permute-start | bytes 1179656 | tf_op jit(solution)/shard_map/ppermute | solution.py:242
  291.5 204.8 %collective-permute-start.12 = (bf16[384,3584]{1,0:T(8,128)(2,1)}, bf16[384,3584]{1,0:T(8,128)(2,1)S(1)}, u32[]{:S(2)}, u32[]{:S(2)}) collective-permute-start(bf16[384,3584]{1,0:T(8,128)(2,1)} %get-tuple-element.18.mine_ref), channel_id=1, source_target_pairs={{0,2},{2,0},{1,3},{3,1},{4,6},{6,4},{5,7},{7,5}} | collective-permute-start | bytes 8257544 | tf_op jit(solution)/shard_map/ppermute | solution.py:242
  291.7 207.1 %copy-start.3 = (bf16[384,1024]{1,0:T(8,128)(2,1)}, bf16[384,1024]{1,0:T(8,128)(2,1)S(1)}, u32[]{:S(2)}) copy-start(bf16[384,1024]{1,0:T(8,128)(2,1)S(1)} %collective-permute-done.16.passed_ref) | copy-start | bytes 2359300
  291.8 207.1 %collective-permute-start.10 = (bf16[384,3584]{1,0:T(8,128)(2,1)}, bf16[384,3584]{1,0:T(8,128)(2,1)}, u32[]{:S(2)}, u32[]{:S(2)}) collective-permute-start(bf16[384,3584]{1,0:T(8,128)(2,1)} %get-tuple-element.17.mine_ref), channel_id=1, source_target_pairs={{0,2},{2,0},{1,3},{3,1},{4,6},{6,4},{5,7},{7,5}} | collective-permute-start | bytes 8257544 | tf_op jit(solution)/shard_map/ppermute | solution.py:242
  293.5 205.4 %collective-permute-start.8 = (bf16[384,3584]{1,0:T(8,128)(2,1)}, bf16[384,3584]{1,0:T(8,128)(2,1)}, u32[]{:S(2)}, u32[]{:S(2)}) collective-permute-start(bf16[384,3584]{1,0:T(8,128)(2,1)} %get-tuple-element.16.mine_ref), channel_id=1, source_target_pairs={{0,2},{2,0},{1,3},{3,1},{4,6},{6,4},{5,7},{7,5}} | collective-permute-start | bytes 8257544 | tf_op jit(solution)/shard_map/ppermute | solution.py:242
  293.8 205.0 %copy-start.2 = (bf16[384,1536]{1,0:T(8,128)(2,1)}, bf16[384,1536]{1,0:T(8,128)(2,1)S(1)}, u32[]{:S(2)}) copy-start(bf16[384,1536]{1,0:T(8,128)(2,1)S(1)} %collective-permute-done.17.passed_ref) | copy-start | bytes 3538948
  293.8 202.0 %collective-permute-start.6 = (bf16[384,1536]{1,0:T(8,128)(2,1)}, bf16[384,1536]{1,0:T(8,128)(2,1)}, u32[]{:S(2)}, u32[]{:S(2)}) collective-permute-start(bf16[384,1536]{1,0:T(8,128)(2,1)} %get-tuple-element.15.mine_ref), channel_id=1, source_target_pairs={{0,2},{2,0},{1,3},{3,1},{4,6},{6,4},{5,7},{7,5}} | collective-permute-start | bytes 3538952 | tf_op jit(solution)/shard_map/ppermute | solution.py:242
  495.8 5.4 collective-permute-start.19
  495.8 3.0 copy-start.1
  495.8 9.4 %collective-permute-start.18 = (bf16[384,3584]{1,0:T(8,128)(2,1)}, bf16[384,3584]{1,0:T(8,128)(2,1)}, u32[]{:S(2)}, u32[]{:S(2)}) collective-permute-start(bf16[384,3584]{1,0:T(8,128)(2,1)} %get-tuple-element.16.mine_ref), channel_id=1, source_target_pairs={{0,1},{1,0},{2,3},{3,2},{4,5},{5,4},{6,7},{7,6}} | collective-permute-start | bytes 8257544 | tf_op jit(solution)/shard_map/ppermute | solution.py:242
  498.3 10.8 %collective-permute-start.13 = (bf16[384,3584]{1,0:T(8,128)(2,1)S(1)}, bf16[384,3584]{1,0:T(8,128)(2,1)}, u32[]{:S(2)}, u32[]{:S(2)}) collective-permute-start(bf16[384,3584]{1,0:T(8,128)(2,1)S(1)} %collective-permute-done.12.mine_ref), channel_id=1, source_target_pairs={{0,1},{1,0},{2,3},{3,2},{4,5},{5,4},{6,7},{7,6}} | collective-permute-start | bytes 8257544 | tf_op jit(solution)/shard_map/ppermute | solution.py:242
  498.8 14.2 %collective-permute-start.11 = (bf16[384,3584]{1,0:T(8,128)(2,1)}, bf16[384,3584]{1,0:T(8,128)(2,1)}, u32[]{:S(2)}, u32[]{:S(2)}) collective-permute-start(bf16[384,3584]{1,0:T(8,128)(2,1)} %collective-permute-done.10.mine_ref), channel_id=1, source_target_pairs={{0,1},{1,0},{2,3},{3,2},{4,5},{5,4},{6,7},{7,6}} | collective-permute-start | bytes 8257544 | tf_op jit(solution)/shard_map/ppermute | solution.py:242
  498.9 83.6 %collective-permute-start.9 = (bf16[384,3584]{1,0:T(8,128)(2,1)}, bf16[384,3584]{1,0:T(8,128)(2,1)}, u32[]{:S(2)}, u32[]{:S(2)}) collective-permute-start(bf16[384,3584]{1,0:T(8,128)(2,1)} %collective-permute-done.8.mine_ref), channel_id=1, source_target_pairs={{0,1},{1,0},{2,3},{3,2},{4,5},{5,4},{6,7},{7,6}} | collective-permute-start | bytes 8257544 | tf_op jit(solution)/shard_map/ppermute | solution.py:242
  501.2 92.0 %collective-permute-start.7 = (bf16[384,1536]{1,0:T(8,128)(2,1)}, bf16[384,1536]{1,0:T(8,128)(2,1)}, u32[]{:S(2)}, u32[]{:S(2)}) collective-permute-start(bf16[384,1536]{1,0:T(8,128)(2,1)} %collective-permute-done.6.mine_ref), channel_id=1, source_target_pairs={{0,1},{1,0},{2,3},{3,2},{4,5},{5,4},{6,7},{7,6}} | collective-permute-start | bytes 3538952 | tf_op jit(solution)/shard_map/ppermute | solution.py:242
  505.2 93.8 %collective-permute-start.5 = (bf16[384,1024]{1,0:T(8,128)(2,1)}, bf16[384,1024]{1,0:T(8,128)(2,1)}, u32[]{:S(2)}, u32[]{:S(2)}) collective-permute-start(bf16[384,1024]{1,0:T(8,128)(2,1)} %collective-permute-done.4.mine_ref), channel_id=1, source_target_pairs={{0,1},{1,0},{2,3},{3,2},{4,5},{5,4},{6,7},{7,6}} | collective-permute-start | bytes 2359304 | tf_op jit(solution)/shard_map/ppermute | solution.py:242
  509.1 94.3 %collective-permute-start.3 = (bf16[384,512]{1,0:T(8,128)(2,1)}, bf16[384,512]{1,0:T(8,128)(2,1)}, u32[]{:S(2)}, u32[]{:S(2)}) collective-permute-start(bf16[384,512]{1,0:T(8,128)(2,1)} %collective-permute-done.2.mine_ref), channel_id=1, source_target_pairs={{0,1},{1,0},{2,3},{3,2},{4,5},{5,4},{6,7},{7,6}} | collective-permute-start | bytes 1179656 | tf_op jit(solution)/shard_map/ppermute | solution.py:242
  513.0 93.1 %collective-permute-start.1 = (bf16[384,512]{1,0:T(8,128)(2,1)}, bf16[384,512]{1,0:T(8,128)(2,1)}, u32[]{:S(2)}, u32[]{:S(2)}) collective-permute-start(bf16[384,512]{1,0:T(8,128)(2,1)} %collective-permute-done.mine_ref), channel_id=1, source_target_pairs={{0,1},{1,0},{2,3},{3,2},{4,5},{5,4},{6,7},{7,6}} | collective-permute-start | bytes 1179656 | tf_op jit(solution)/shard_map/ppermute | solution.py:242
  (3 other events, 3.5 us)

commit v4 on v3

--- a/solution.py
+++ b/solution.py
@@ -30,20 +30,21 @@
     core, x = lax.rem(me, 2), lax.div(me, 2)
     sibling, across = 2 * x + 1 - core, 2 * (1 - x) + core
 
-    def load_a(n, side):
-        first = pl.multiple_of(half * jnp.where(side == 0, 1 - core, core), half)
+    def load_a(n, part):
+        owner = core if part % 2 else 1 - core
+        first = pl.multiple_of(half * owner + quarter * (1 - x if part < 2 else x), quarter)
         s = lax.rem(n, 2)
-        return pltpu.make_async_copy(a.at[0, n, :, pl.ds(first, half)], abuf.at[s, side], a_sem.at[s, side])
+        return pltpu.make_async_copy(a.at[0, n, :, pl.ds(first, quarter)], abuf.at[s, part], a_sem.at[s, part])
 
     def load_g(t):
         n, j = lax.div(t, per), lax.rem(t, per)
         s = lax.rem(t, 2)
         return pltpu.make_async_copy(g.at[0, n, :, pl.ds(pl.multiple_of(j * CT, CT), CT)], gbuf.at[s], g_sem.at[s])
 
-    def send_term(t):
+    def send_term(t, q):
         s = lax.rem(t, 2)
         return pltpu.make_async_remote_copy(
-            tsend.at[s], term.at[s], ts_sem.at[s], tr_sem.at[s], device_id={"dp": sibling}, device_id_type=MESH
+            tsend.at[s, q], term.at[s, q], ts_sem.at[s, q], tr_sem.at[s, q], device_id={"dp": sibling}, device_id_type=MESH
         )
 
     def send_x(t):
@@ -75,19 +76,6 @@
             @pl.when((u >= lo) & (u < lo + c // CT))
             def _():
                 store_f(u, out, c0).start()
-
-    def own_sum(t):
-        send_term(t).wait_recv()
-
-        @pl.when(t >= SENDS)
-        def _():
-            send_x(t - SENDS).wait_send()
-
-        rows = [pl.ds(pl.multiple_of(quarter * q, quarter), quarter) for q in (x, 1 - x)]
-        s = lax.rem(t, 2)
-        own[lax.rem(t, KEPT)] = pend[rows[0], :] + term[s, rows[0], :].astype(jnp.float32)
-        xsend[lax.rem(t, SENDS)] = (pend[rows[1], :] + term[s, rows[1], :].astype(jnp.float32)).astype(xsend.dtype)
-        send_x(t).start()
 
     load_a(0, 0).start()
     load_g(0).start()
@@ -100,46 +88,54 @@
         n, j = lax.div(t, per), lax.rem(t, per)
         s, sa = lax.rem(t, 2), lax.rem(n, 2)
 
-        @pl.when(j == 0)
-        def _():
-            load_a(n, 0).wait()
+        def need_a(part):
+            @pl.when(j == 0)
+            def _():
+                load_a(n, part).wait()
+
+            if part < 3:
+                @pl.when(t == 0)
+                def _():
+                    load_a(0, part + 1).start()
 
         load_g(t).wait()
 
-        @pl.when(t == 0)
-        def _():
-            load_a(0, 1).start()
-
-        @pl.when(t + 1 < tiles)
+        @pl.when((t > 0) & (t + 1 < tiles))
         def _():
             load_g(t + 1).start()
 
         @pl.when((j == 1) & (n + 1 < matrices))
         def _():
-            load_a(n + 1, 0).start()
-            load_a(n + 1, 1).start()
-
-        @pl.when(t >= 2)
-        def _():
-            send_term(t - 2).wait_send()
-
-        tsend[s] = _dot(abuf[sa, 0], gbuf[s]).astype(tsend.dtype)
-
-        @pl.when(t >= 2)
-        def _():
-            own_sum(t - 1)
-
-        send_term(t).start()
-
-        @pl.when(j == 0)
-        def _():
-            load_a(n, 1).wait()
-
-        pend[...] = _dot(abuf[sa, 1], gbuf[s])
-
-        @pl.when(t == 0)
-        def _():
-            own_sum(0)
+            for part in range(4):
+                load_a(n + 1, part).start()
+
+        for q in range(2):
+            need_a(2 * q)
+
+            @pl.when(t >= 2)
+            def _():
+                send_term(t - 2, q).wait_send()
+
+            tsend[s, q] = _dot(abuf[sa, 2 * q], gbuf[s]).astype(tsend.dtype)
+            send_term(t, q).start()
+            need_a(2 * q + 1)
+            pend[...] = _dot(abuf[sa, 2 * q + 1], gbuf[s])
+            send_term(t, q).wait_recv()
+            total = pend[...] + term[s, q].astype(jnp.float32)
+            if q == 1:
+                own[lax.rem(t, KEPT)] = total
+                continue
+
+            @pl.when(t >= SENDS)
+            def _():
+                send_x(t - SENDS).wait_send()
+
+            xsend[lax.rem(t, SENDS)] = total.astype(xsend.dtype)
+            send_x(t).start()
+
+            @pl.when(t == 0)
+            def _():
+                load_g(1).start()
 
         @pl.when(t >= LAG)
         def _():
@@ -148,7 +144,6 @@
         return 0
 
     lax.fori_loop(0, tiles, step, 0)
-    own_sum(tiles - 1)
 
     def rest(u, _):
         finish(u)
@@ -162,13 +157,14 @@
 
     lax.fori_loop(tiles - SENDS, tiles, drain, 0)
     for t in (tiles - 2, tiles - 1):
-        send_term(t).wait_send()
+        for q in range(2):
+            send_term(t, q).wait_send()
         wait_f(t)
 
 
 def reduce_to_quarters(a, g):
     _, matrices, k, d = a.shape
-    half, quarter, tiles = d // 2, d // 4, matrices * (g.shape[3] // CT)
+    quarter, tiles = d // 4, matrices * (g.shape[3] // CT)
     flops = 2 * k * d * g.shape[3] * matrices
     return pl.pallas_call(
         reduce_kernel,
@@ -176,19 +172,19 @@
         in_specs=[ANY] * 2,
         out_specs=(ANY,) * len(PIECES),
         scratch_shapes=[
-            pltpu.VMEM((2, 2, k, half), jnp.bfloat16),
+            pltpu.VMEM((2, 4, k, quarter), jnp.bfloat16),
             pltpu.VMEM((2, k, CT), jnp.bfloat16),
-            pltpu.VMEM((2, half, CT), jnp.bfloat16),
-            pltpu.VMEM((2, half, CT), jnp.bfloat16),
-            pltpu.VMEM((half, CT), jnp.float32),
+            pltpu.VMEM((2, 2, quarter, CT), jnp.bfloat16),
+            pltpu.VMEM((2, 2, quarter, CT), jnp.bfloat16),
+            pltpu.VMEM((quarter, CT), jnp.float32),
             pltpu.VMEM((SENDS, quarter, CT), jnp.bfloat16),
             pltpu.VMEM((KEPT, quarter, CT), jnp.float32),
             pltpu.VMEM((tiles, quarter, CT), jnp.bfloat16),
             pltpu.VMEM((2, quarter, CT), jnp.bfloat16),
+            pltpu.SemaphoreType.DMA((2, 4)),
+            pltpu.SemaphoreType.DMA((2,)),
             pltpu.SemaphoreType.DMA((2, 2)),
-            pltpu.SemaphoreType.DMA((2,)),
-            pltpu.SemaphoreType.DMA((2,)),
-            pltpu.SemaphoreType.DMA((2,)),
+            pltpu.SemaphoreType.DMA((2, 2)),
             pltpu.SemaphoreType.DMA((SENDS,)),
             pltpu.SemaphoreType.DMA((tiles,)),
             pltpu.SemaphoreType.DMA((2,)),

time: 611 us -> 605 us (level)
  no operation moved by 1% of the time
where the time goes in v4:
time: 605 us; the launch traced here: 603 us
  Pallas kernels  344 us (57%)
  waiting for transfers between devices  246 us (41%)
  starting transfers between devices  9.14 us (2%)
    pallas_call x1, Pallas kernels, reduce_to_quarters(): pl.pallas_call(reduce_kernel, out_shape=tuple((jax.ShapeDtypeStruct((quar...  249 us
    ppermute x21, waiting for transfers between devices, swap(): return lax.ppermute(t, 'dp', pairs)  246 us
    pallas_call x14, Pallas kernels, place(): pl.pallas_call(body, out_shape=jax.ShapeDtypeStruct(shape, jnp.bfloat16),...  95.6 us
  transfers between devices with their start and end apart: 21, of which 7 were waited for; matrix products, arithmetic and copies ran while one was open for 0% of the time, Pallas kernels for 15%

profile of v4, /device:TPU:0, one launch (start us, length us, event | category | flops | bytes accessed | tf_op | source)
XLA Modules:
  0.0 603.3 jit_solution(14497358614661564253)
XLA Ops:
  0.0 248.8 %reduce.1 = (bf16[384,3584]{1,0:T(8,128)(2,1)}, bf16[384,3584]{1,0:T(8,128)(2,1)}, bf16[384,3584]{1,0:T(8,128)(2,1)}, bf16[384,1536]{1,0:T(8,128)(2,1)}, bf16[38...) custom-call(bf16[1,4,4096,1536]{3,2,1,0:T(8,128)(2,1)} %a.1, bf16[1,4,4096,3584]{3,2,1,0:T(8,128)(2,1)} %g.1), custom_call_target="tpu_custom_call" | custom-call | flops 180388626432 | bytes 167772160 | tf_op jit(solution)/shard_map/reduce/pallas_call | solution.py:169
  249.3 2.0 collective-permute-start.4
  253.1 8.5 %collective-permute-done.2.mine_ref = bf16[384,512]{1,0:T(8,128)(2,1)} collective-permute-done((bf16[384,512]{1,0:T(8,128)(2,1)}, bf16[384,512]{1,0:T(8,128)(2,1)}, u32[]{:S(2)}, u32[]{:S(2)}) %collective-permute-start.2) | collective-permute-done | bytes 393248 | tf_op jit(solution)/shard_map/ppermute | solution.py:238
  261.6 24.3 %collective-permute-done.mine_ref = bf16[384,512]{1,0:T(8,128)(2,1)} collective-permute-done((bf16[384,512]{1,0:T(8,128)(2,1)}, bf16[384,512]{1,0:T(8,128)(2,1)}, u32[]{:S(2)}, u32[]{:S(2)}) %collective-permute-start) | collective-permute-done | bytes 393248 | tf_op jit(solution)/shard_map/ppermute | solution.py:238
  290.0 200.3 %collective-permute-done.6.mine_ref = bf16[384,1536]{1,0:T(8,128)(2,1)} collective-permute-done((bf16[384,1536]{1,0:T(8,128)(2,1)}, bf16[384,1536]{1,0:T(8,128)(2,1)}, u32[]{:S(2)}, u32[]{:S(2)}) %collective-permute-start.6) | collective-permute-done | bytes 1179680 | tf_op jit(solution)/shard_map/ppermute | solution.py:238
  490.8 2.0 copy-done
  493.9 1.9 collective-permute-done.19.passed_ref
  495.9 3.8 collective-permute-done.18.passed_ref
  500.4 3.2 collective-permute-done.13.passed_ref
  503.7 3.8 collective-permute-done.11.passed_ref
  507.7 10.7 %shard_map.28.rest_0_ = bf16[4,1536,3584]{2,1,0:T(8,128)(2,1)} custom-call(s32[2]{0:T(128)} %pad_add_fusion.pos.dep_ref, bf16[384,3584]{1,0:T(8,128)(2,1)} %get-tuple-element.18.mine_ref, bf16[384,3584]{1,0:T(8,128)(2,1)} %copy-done.1, s32[2]{0:T(128)} %pad_add_fusion.pos.dep_ref), custom_call_target="tpu_custom_call" | custom-call | flops 550502400 | bytes 11010048 | tf_op jit(solution)/shard_map/pallas_call | solution.py:214
  518.4 10.7 %shard_map.29.rest_0_ = bf16[4,1536,3584]{2,1,0:T(8,128)(2,1)} custom-call(s32[2]{0:T(128)} %pad_add_fusion.pos.dep_ref, bf16[384,3584]{1,0:T(8,128)(2,1)} %get-tuple-element.17.mine_ref, bf16[384,3584]{1,0:T(8,128)(2,1)} %collective-permute-done.19.passed_ref, s32[2]{0:T(128)} %pad_add_fusion.pos.dep_ref, ...), custom_call_target="tpu_custom_call", output_to_operand_aliasing={{}: (4, {})} | custom-call | flops 550502400 | bytes 11010048 | tf_op jit(solution)/shard_map/pallas_call | solution.py:214
  529.1 10.7 %shard_map.30.rest_0_ = bf16[4,1536,3584]{2,1,0:T(8,128)(2,1)} custom-call(s32[2]{0:T(128)} %pad_add_fusion.pos.dep_ref, bf16[384,3584]{1,0:T(8,128)(2,1)} %get-tuple-element.16.mine_ref, bf16[384,3584]{1,0:T(8,128)(2,1)} %collective-permute-done.18.passed_ref, s32[2]{0:T(128)} %pad_add_fusion.pos.dep_ref, ...), custom_call_target="tpu_custom_call", output_to_operand_aliasing={{}: (4, {})} | custom-call | flops 550502400 | bytes 11010048 | tf_op jit(solution)/shard_map/pallas_call | solution.py:214
  539.9 5.7 shard_map.31.rest_0_
  545.6 4.5 shard_map.32.rest_0_
  550.1 2.7 shard_map.33.rest_0_
  552.8 2.7 shard_map.34.rest_0_
  555.5 10.7 %shard_map.35.rest_0_ = bf16[4,1536,3584]{2,1,0:T(8,128)(2,1)} custom-call(s32[2]{0:T(128)} %pad_add_fusion.pos.dep_ref, bf16[384,3584]{1,0:T(8,128)(2,1)} %copy-done, bf16[384,3584]{1,0:T(8,128)(2,1)} %collective-permute-done.13.passed_ref, s32[2]{0:T(128)} %pad_add_fusion.pos.dep_ref, ...), custom_call_target="tpu_custom_call", output_to_operand_aliasing={{}: (4, {})} | custom-call | flops 550502400 | bytes 11010048 | tf_op jit(solution)/shard_map/pallas_call | solution.py:214
  566.2 10.7 %shard_map.36.rest_0_ = bf16[4,1536,3584]{2,1,0:T(8,128)(2,1)} custom-call(s32[2]{0:T(128)} %pad_add_fusion.pos.dep_ref, bf16[384,3584]{1,0:T(8,128)(2,1)} %collective-permute-done.10.mine_ref, bf16[384,3584]{1,0:T(8,128)(2,1)} %collective-permute-done.11.passed_ref, s32[2]{0:T(128)} %pad_add_fusion.pos.dep_ref, ...), custom_call_target="tpu_custom_call", output_to_operand_aliasing={{}: (4, {})} | custom-call | flops 550502400 | bytes 11010048 | tf_op jit(solution)/shard_map/pallas_call | solution.py:214
  576.9 10.7 %shard_map.37.rest_0_ = bf16[4,1536,3584]{2,1,0:T(8,128)(2,1)} custom-call(s32[2]{0:T(128)} %pad_add_fusion.pos.dep_ref, bf16[384,3584]{1,0:T(8,128)(2,1)} %collective-permute-done.8.mine_ref, bf16[384,3584]{1,0:T(8,128)(2,1)} %collective-permute-done.9.passed_ref, s32[2]{0:T(128)} %pad_add_fusion.pos.dep_ref, ...), custom_call_target="tpu_custom_call", output_to_operand_aliasing={{}: (4, {})} | custom-call | flops 550502400 | bytes 11010048 | tf_op jit(solution)/shard_map/pallas_call | solution.py:214
  587.7 5.7 shard_map.38.rest_0_
  593.4 4.5 shard_map.39.rest_0_
  597.9 2.7 shard_map.40.rest_0_
  600.6 2.7 shard_map.41
  (46 shorter events, 9.1 us)
Async XLA Ops:
  248.8 2.6 collective-permute-start.15
  248.8 2.8 collective-permute-start.14
  249.3 12.3 %collective-permute-start.2 = (bf16[384,512]{1,0:T(8,128)(2,1)}, bf16[384,512]{1,0:T(8,128)(2,1)}, u32[]{:S(2)}, u32[]{:S(2)}) collective-permute-start(bf16[384,512]{1,0:T(8,128)(2,1)} %get-tuple-element.13.mine_ref), channel_id=1, source_target_pairs={{0,2},{2,0},{1,3},{3,1},{4,6},{6,4},{5,7},{7,5}} | collective-permute-start | bytes 1179656 | tf_op jit(solution)/shard_map/ppermute | solution.py:238
  249.3 36.9 %collective-permute-start.16 = (bf16[384,1024]{1,0:T(8,128)(2,1)}, bf16[384,1024]{1,0:T(8,128)(2,1)S(1)}, u32[]{:S(2)}, u32[]{:S(2)}) collective-permute-start(bf16[384,1024]{1,0:T(8,128)(2,1)} %get-tuple-element.14.mine_ref), channel_id=1, source_target_pairs={{0,1},{1,0},{2,3},{3,2},{4,5},{5,4},{6,7},{7,6}} | collective-permute-start | bytes 2359304 | tf_op jit(solution)/shard_map/ppermute | solution.py:238
  249.3 38.6 %collective-permute-start.4 = (bf16[384,1024]{1,0:T(8,128)(2,1)}, bf16[384,1024]{1,0:T(8,128)(2,1)}, u32[]{:S(2)}, u32[]{:S(2)}) collective-permute-start(bf16[384,1024]{1,0:T(8,128)(2,1)} %get-tuple-element.14.mine_ref), channel_id=1, source_target_pairs={{0,2},{2,0},{1,3},{3,1},{4,6},{6,4},{5,7},{7,5}} | collective-permute-start | bytes 2359304 | tf_op jit(solution)/shard_map/ppermute | solution.py:238
  251.3 36.9 %collective-permute-start.17 = (bf16[384,1536]{1,0:T(8,128)(2,1)}, bf16[384,1536]{1,0:T(8,128)(2,1)S(1)}, u32[]{:S(2)}, u32[]{:S(2)}) collective-permute-start(bf16[384,1536]{1,0:T(8,128)(2,1)} %get-tuple-element.15.mine_ref), channel_id=1, source_target_pairs={{0,1},{1,0},{2,3},{3,2},{4,5},{5,4},{6,7},{7,6}} | collective-permute-start | bytes 3538952 | tf_op jit(solution)/shard_map/ppermute | solution.py:238
  252.9 237.4 %collective-permute-start.20 = (bf16[384,3584]{1,0:T(8,128)(2,1)}, bf16[384,3584]{1,0:T(8,128)(2,1)S(1)}, u32[]{:S(2)}, u32[]{:S(2)}) collective-permute-start(bf16[384,3584]{1,0:T(8,128)(2,1)} %get-tuple-element.18.mine_ref), channel_id=1, source_target_pairs={{0,1},{1,0},{2,3},{3,2},{4,5},{5,4},{6,7},{7,6}} | collective-permute-start | bytes 8257544 | tf_op jit(solution)/shard_map/ppermute | solution.py:238
  261.6 24.3 %collective-permute-start = (bf16[384,512]{1,0:T(8,128)(2,1)}, bf16[384,512]{1,0:T(8,128)(2,1)}, u32[]{:S(2)}, u32[]{:S(2)}) collective-permute-start(bf16[384,512]{1,0:T(8,128)(2,1)} %get-tuple-element.12.mine_ref), channel_id=1, source_target_pairs={{0,2},{2,0},{1,3},{3,1},{4,6},{6,4},{5,7},{7,5}} | collective-permute-start | bytes 1179656 | tf_op jit(solution)/shard_map/ppermute | solution.py:238
  286.0 204.8 %collective-permute-start.12 = (bf16[384,3584]{1,0:T(8,128)(2,1)}, bf16[384,3584]{1,0:T(8,128)(2,1)S(1)}, u32[]{:S(2)}, u32[]{:S(2)}) collective-permute-start(bf16[384,3584]{1,0:T(8,128)(2,1)} %get-tuple-element.18.mine_ref), channel_id=1, source_target_pairs={{0,2},{2,0},{1,3},{3,1},{4,6},{6,4},{5,7},{7,5}} | collective-permute-start | bytes 8257544 | tf_op jit(solution)/shard_map/ppermute | solution.py:238
  286.2 207.1 %copy-start.3 = (bf16[384,1024]{1,0:T(8,128)(2,1)}, bf16[384,1024]{1,0:T(8,128)(2,1)S(1)}, u32[]{:S(2)}) copy-start(bf16[384,1024]{1,0:T(8,128)(2,1)S(1)} %collective-permute-done.16.passed_ref) | copy-start | bytes 2359300
  286.2 207.1 %collective-permute-start.10 = (bf16[384,3584]{1,0:T(8,128)(2,1)}, bf16[384,3584]{1,0:T(8,128)(2,1)}, u32[]{:S(2)}, u32[]{:S(2)}) collective-permute-start(bf16[384,3584]{1,0:T(8,128)(2,1)} %get-tuple-element.17.mine_ref), channel_id=1, source_target_pairs={{0,2},{2,0},{1,3},{3,1},{4,6},{6,4},{5,7},{7,5}} | collective-permute-start | bytes 8257544 | tf_op jit(solution)/shard_map/ppermute | solution.py:238
  288.0 205.4 %collective-permute-start.8 = (bf16[384,3584]{1,0:T(8,128)(2,1)}, bf16[384,3584]{1,0:T(8,128)(2,1)}, u32[]{:S(2)}, u32[]{:S(2)}) collective-permute-start(bf16[384,3584]{1,0:T(8,128)(2,1)} %get-tuple-element.16.mine_ref), channel_id=1, source_target_pairs={{0,2},{2,0},{1,3},{3,1},{4,6},{6,4},{5,7},{7,5}} | collective-permute-start | bytes 8257544 | tf_op jit(solution)/shard_map/ppermute | solution.py:238
  288.3 205.0 %copy-start.2 = (bf16[384,1536]{1,0:T(8,128)(2,1)}, bf16[384,1536]{1,0:T(8,128)(2,1)S(1)}, u32[]{:S(2)}) copy-start(bf16[384,1536]{1,0:T(8,128)(2,1)S(1)} %collective-permute-done.17.passed_ref) | copy-start | bytes 3538948
  288.3 202.0 %collective-permute-start.6 = (bf16[384,1536]{1,0:T(8,128)(2,1)}, bf16[384,1536]{1,0:T(8,128)(2,1)}, u32[]{:S(2)}, u32[]{:S(2)}) collective-permute-start(bf16[384,1536]{1,0:T(8,128)(2,1)} %get-tuple-element.15.mine_ref), channel_id=1, source_target_pairs={{0,2},{2,0},{1,3},{3,1},{4,6},{6,4},{5,7},{7,5}} | collective-permute-start | bytes 3538952 | tf_op jit(solution)/shard_map/ppermute | solution.py:238
  490.3 5.4 collective-permute-start.19
  490.3 3.0 copy-start.1
  490.3 9.4 %collective-permute-start.18 = (bf16[384,3584]{1,0:T(8,128)(2,1)}, bf16[384,3584]{1,0:T(8,128)(2,1)}, u32[]{:S(2)}, u32[]{:S(2)}) collective-permute-start(bf16[384,3584]{1,0:T(8,128)(2,1)} %get-tuple-element.16.mine_ref), channel_id=1, source_target_pairs={{0,1},{1,0},{2,3},{3,2},{4,5},{5,4},{6,7},{7,6}} | collective-permute-start | bytes 8257544 | tf_op jit(solution)/shard_map/ppermute | solution.py:238
  492.8 10.8 %collective-permute-start.13 = (bf16[384,3584]{1,0:T(8,128)(2,1)S(1)}, bf16[384,3584]{1,0:T(8,128)(2,1)}, u32[]{:S(2)}, u32[]{:S(2)}) collective-permute-start(bf16[384,3584]{1,0:T(8,128)(2,1)S(1)} %collective-permute-done.12.mine_ref), channel_id=1, source_target_pairs={{0,1},{1,0},{2,3},{3,2},{4,5},{5,4},{6,7},{7,6}} | collective-permute-start | bytes 8257544 | tf_op jit(solution)/shard_map/ppermute | solution.py:238
  493.3 14.2 %collective-permute-start.11 = (bf16[384,3584]{1,0:T(8,128)(2,1)}, bf16[384,3584]{1,0:T(8,128)(2,1)}, u32[]{:S(2)}, u32[]{:S(2)}) collective-permute-start(bf16[384,3584]{1,0:T(8,128)(2,1)} %collective-permute-done.10.mine_ref), channel_id=1, source_target_pairs={{0,1},{1,0},{2,3},{3,2},{4,5},{5,4},{6,7},{7,6}} | collective-permute-start | bytes 8257544 | tf_op jit(solution)/shard_map/ppermute | solution.py:238
  493.4 83.6 %collective-permute-start.9 = (bf16[384,3584]{1,0:T(8,128)(2,1)}, bf16[384,3584]{1,0:T(8,128)(2,1)}, u32[]{:S(2)}, u32[]{:S(2)}) collective-permute-start(bf16[384,3584]{1,0:T(8,128)(2,1)} %collective-permute-done.8.mine_ref), channel_id=1, source_target_pairs={{0,1},{1,0},{2,3},{3,2},{4,5},{5,4},{6,7},{7,6}} | collective-permute-start | bytes 8257544 | tf_op jit(solution)/shard_map/ppermute | solution.py:238
  495.7 92.0 %collective-permute-start.7 = (bf16[384,1536]{1,0:T(8,128)(2,1)}, bf16[384,1536]{1,0:T(8,128)(2,1)}, u32[]{:S(2)}, u32[]{:S(2)}) collective-permute-start(bf16[384,1536]{1,0:T(8,128)(2,1)} %collective-permute-done.6.mine_ref), channel_id=1, source_target_pairs={{0,1},{1,0},{2,3},{3,2},{4,5},{5,4},{6,7},{7,6}} | collective-permute-start | bytes 3538952 | tf_op jit(solution)/shard_map/ppermute | solution.py:238
  499.7 93.8 %collective-permute-start.5 = (bf16[384,1024]{1,0:T(8,128)(2,1)}, bf16[384,1024]{1,0:T(8,128)(2,1)}, u32[]{:S(2)}, u32[]{:S(2)}) collective-permute-start(bf16[384,1024]{1,0:T(8,128)(2,1)} %collective-permute-done.4.mine_ref), channel_id=1, source_target_pairs={{0,1},{1,0},{2,3},{3,2},{4,5},{5,4},{6,7},{7,6}} | collective-permute-start | bytes 2359304 | tf_op jit(solution)/shard_map/ppermute | solution.py:238
  503.6 94.3 %collective-permute-start.3 = (bf16[384,512]{1,0:T(8,128)(2,1)}, bf16[384,512]{1,0:T(8,128)(2,1)}, u32[]{:S(2)}, u32[]{:S(2)}) collective-permute-start(bf16[384,512]{1,0:T(8,128)(2,1)} %collective-permute-done.2.mine_ref), channel_id=1, source_target_pairs={{0,1},{1,0},{2,3},{3,2},{4,5},{5,4},{6,7},{7,6}} | collective-permute-start | bytes 1179656 | tf_op jit(solution)/shard_map/ppermute | solution.py:238
  507.5 93.1 %collective-permute-start.1 = (bf16[384,512]{1,0:T(8,128)(2,1)}, bf16[384,512]{1,0:T(8,128)(2,1)}, u32[]{:S(2)}, u32[]{:S(2)}) collective-permute-start(bf16[384,512]{1,0:T(8,128)(2,1)} %collective-permute-done.mine_ref), channel_id=1, source_target_pairs={{0,1},{1,0},{2,3},{3,2},{4,5},{5,4},{6,7},{7,6}} | collective-permute-start | bytes 1179656 | tf_op jit(solution)/shard_map/ppermute | solution.py:238
  (3 other events, 3.5 us)

commit v5 on v4

v5 whole, which is shorter than its diff:
```python
import jax
import jax.numpy as jnp
from jax import lax
from jax.experimental import pallas as pl
from jax.experimental.pallas import tpu as pltpu
from jax.sharding import PartitionSpec as P


CT = 512
SENDS = 8
PIECES = ((0, 0, 512), (0, 512, 3072), (1, 0, 3584), (2, 0, 3584), (3, 0, 1536), (3, 1536, 1024), (3, 2560, 512), (3, 3072, 512))
VMEM = 67043328
ANY = pl.BlockSpec(memory_space=pl.ANY)
MESH = pl.DeviceIdType.MESH


def _dot(a, g):
    return lax.dot_general(a, g, (((0,), (0,)), ((), ())), preferred_element_type=jnp.float32)


def reduce_kernel(a, g, *refs):
    outs, z0, scratch = refs[: len(PIECES)], refs[len(PIECES)], refs[len(PIECES) + 1 :]
    abuf, gbuf, tsend, term, pend, xsend, got, fbuf, first_f = scratch[:9]
    a_sem, g_sem, ts_sem, tr_sem, xs_sem, xr_sem, f_sem, z_sem = scratch[9:]
    _, matrices, _, d = a.shape
    half, quarter, per = d // 2, d // 4, g.shape[3] // CT
    tiles = matrices * per
    steps = 2 * tiles
    me = lax.axis_index("dp")
    core, x = lax.rem(me, 2), lax.div(me, 2)
    sibling, across = 2 * x + 1 - core, 2 * (1 - x) + core
    halves = [pl.ds(h * (CT // 2), CT // 2) for h in range(2)]

    def load_a(n, part):
        owner = core if part % 2 else 1 - core
        first = pl.multiple_of(half * owner + quarter * (1 - x if part < 2 else x), quarter)
        s = lax.rem(n, 2)
        return pltpu.make_async_copy(a.at[0, n, :, pl.ds(first, quarter)], abuf.at[s, part], a_sem.at[s, part])

    def turn(i):
        k = i - per
        alone = (i < per) | (i >= steps - per)
        p = jnp.where(alone, jnp.where(i < per, 0, 1), 1 - lax.rem(k + 2 * per, 2))
        t = jnp.where(alone, jnp.where(i < per, i, i - tiles), jnp.where(p == 0, per + lax.div(k, 2), lax.div(k, 2)))
        return p, t

    def load_g(i):
        _, t = turn(i)
        n, j = lax.div(t, per), lax.rem(t, per)
        s = lax.rem(i, 2)
        return pltpu.make_async_copy(g.at[0, n, :, pl.ds(pl.multiple_of(j * CT, CT), CT)], gbuf.at[s], g_sem.at[s])

    def load_first_g(h):
        return pltpu.make_async_copy(g.at[0, 0, :, halves[h]], gbuf.at[0, :, halves[h]], g_sem.at[2 * h])

    def to(other, src, dst, send_sem, recv_sem):
        return pltpu.make_async_remote_copy(src, dst, send_sem, recv_sem, device_id={"dp": other}, device_id_type=MESH)

    def send_term(i):
        s = lax.rem(i, 2)
        return to(sibling, tsend.at[s], term.at[s], ts_sem.at[s], tr_sem.at[s])

    def send_first_term(h):
        return to(sibling, tsend.at[0, :, halves[h]], term.at[0, :, halves[h]], ts_sem.at[2 * h], tr_sem.at[2 * h])

    def send_x(t):
        s = lax.rem(t, SENDS)
        return to(across, xsend.at[s], got.at[t], xs_sem.at[s], xr_sem.at[t])

    def send_first_x(h):
        return to(across, xsend.at[0, :, halves[h]], got.at[0, :, halves[h]], xs_sem.at[SENDS * h], xr_sem.at[tiles * h])

    def send_z():
        return to(across, first_f, z0, z_sem.at[0], z_sem.at[1])

    def store_f(u, out, c0):
        s = lax.rem(u, 2)
        at = pl.multiple_of(lax.rem(u, per) * CT - c0, CT)
        return pltpu.make_async_copy(fbuf.at[s], out.at[:, pl.ds(at, CT)], f_sem.at[s])

    def wait_f(u):
        s = lax.rem(u, 2)
        pltpu.make_async_copy(fbuf.at[s], outs[0].at[:, pl.ds(0, CT)], f_sem.at[s]).wait()

    def finish(u, s):
        @pl.when(u == 0)
        def _():
            for h in range(2):
                send_first_x(h).wait_recv()

        @pl.when(u > 0)
        def _():
            send_x(u).wait_recv()

        @pl.when(u >= 2)
        def _():
            wait_f(u - 2)

        f = (pend[...] + term[s].astype(jnp.float32) + got[u].astype(jnp.float32)).astype(fbuf.dtype)
        fbuf[lax.rem(u, 2)] = f

        @pl.when(u == 0)
        def _():
            first_f[...] = f

        for (n, c0, c), out in zip(PIECES, outs):
            lo = n * per + c0 // CT

            @pl.when((u >= lo) & (u < lo + c // CT))
            def _():
                store_f(u, out, c0).start()

    load_a(0, 0).start()
    load_first_g(0).start()
    barrier = pltpu.get_barrier_semaphore()
    for other in (sibling, across):
        pl.semaphore_signal(barrier, inc=1, device_id={"dp": other}, device_id_type=MESH)
    pl.semaphore_wait(barrier, 2)

    for h in range(2):
        if h == 0:
            load_a(0, 0).wait()
        load_first_g(h).wait()
        if h == 0:
            load_a(0, 1).start()
            load_first_g(1).start()
        else:
            load_g(1).start()
        tsend[0, :, halves[h]] = _dot(abuf[0, 0], gbuf[0, :, halves[h]]).astype(tsend.dtype)
        send_first_term(h).start()
        if h == 0:
            load_a(0, 1).wait()
        pend[:, halves[h]] = _dot(abuf[0, 1], gbuf[0, :, halves[h]])
        send_first_term(h).wait_recv()
        xsend[0, :, halves[h]] = (pend[:, halves[h]] + term[0, :, halves[h]].astype(jnp.float32)).astype(xsend.dtype)
        send_first_x(h).start()

    def step(i, _):
        p, t = turn(i)
        n, j = lax.div(t, per), lax.rem(t, per)
        s, sa = lax.rem(i, 2), lax.rem(n, 2)

        for q in range(2):

            @pl.when((p == q) & (j == 0))
            def _():
                load_a(n, 2 * q).wait()
                load_a(n, 2 * q + 1).wait()

            @pl.when((p == q) & (j == 2) & (n + 1 < matrices))
            def _():
                load_a(n + 1, 2 * q).start()
                load_a(n + 1, 2 * q + 1).start()

        load_g(i).wait()

        @pl.when(i + 1 < steps)
        def _():
            load_g(i + 1).start()

        @pl.when(i == 1)
        def _():
            for part in (2, 3):
                load_a(0, part).start()

        @pl.when(i == 2)
        def _():
            for h in range(2):
                send_first_term(h).wait_send()

        @pl.when(i > 2)
        def _():
            send_term(i - 2).wait_send()

        tsend[s] = _dot(abuf[sa, 2 * p], gbuf[s]).astype(tsend.dtype)
        send_term(i).start()
        pend[...] = _dot(abuf[sa, 2 * p + 1], gbuf[s])
        send_term(i).wait_recv()

        @pl.when(p == 0)
        def _():
            @pl.when(t == SENDS)
            def _():
                for h in range(2):
                    send_first_x(h).wait_send()

            @pl.when(t > SENDS)
            def _():
                send_x(t - SENDS).wait_send()

            xsend[lax.rem(t, SENDS)] = (pend[...] + term[s].astype(jnp.float32)).astype(xsend.dtype)
            send_x(t).start()

            @pl.when(t == tiles - 1)
            def _():
                send_z().start()

        @pl.when(p == 1)
        def _():
            finish(t, s)

        return 0

    lax.fori_loop(1, steps, step, 0)

    def drain(t, _):
        send_x(t).wait_send()
        return 0

    lax.fori_loop(tiles - SENDS, tiles, drain, 0)
    for i in (steps - 2, steps - 1):
        send_term(i).wait_send()
    for u in (tiles - 2, tiles - 1):
        wait_f(u)
    send_z().wait()


def reduce_to_quarters(a, g):
    _, matrices, k, d = a.shape
    quarter, tiles = d // 4, matrices * (g.shape[3] // CT)
    flops = 2 * k * d * g.shape[3] * matrices
    return pl.pallas_call(
        reduce_kernel,
        out_shape=tuple(jax.ShapeDtypeStruct((quarter, c), jnp.bfloat16) for c in [c for _, _, c in PIECES] + [CT]),
        in_specs=[ANY] * 2,
        out_specs=(ANY,) * (len(PIECES) + 1),
        scratch_shapes=[
            pltpu.VMEM((2, 4, k, quarter), jnp.bfloat16),
            pltpu.VMEM((2, k, CT), jnp.bfloat16),
            pltpu.VMEM((2, quarter, CT), jnp.bfloat16),
            pltpu.VMEM((2, quarter, CT), jnp.bfloat16),
            pltpu.VMEM((quarter, CT), jnp.float32),
            pltpu.VMEM((SENDS, quarter, CT), jnp.bfloat16),
            pltpu.VMEM((tiles, quarter, CT), jnp.bfloat16),
            pltpu.VMEM((2, quarter, CT), jnp.bfloat16),
            pltpu.VMEM((quarter, CT), jnp.bfloat16),
            pltpu.SemaphoreType.DMA((2, 4)),
            pltpu.SemaphoreType.DMA((3,)),
            pltpu.SemaphoreType.DMA((3,)),
            pltpu.SemaphoreType.DMA((3,)),
            pltpu.SemaphoreType.DMA((SENDS + 1,)),
            pltpu.SemaphoreType.DMA((tiles + 1,)),
            pltpu.SemaphoreType.DMA((2,)),
            pltpu.SemaphoreType.DMA((2,)),
        ],
        name="reduce",
        compiler_params=pltpu.CompilerParams(vmem_limit_bytes=VMEM, collective_id=0, has_side_effects=True),
        cost_estimate=pl.CostEstimate(flops=flops, bytes_accessed=2 * a.size + 2 * g.size, transcendentals=0),
    )(a, g)


def place(pos, mine, passed, out, dep, shape, n, c0, c, other_chip):
    quarter, ct = mine.shape[0], min(c, 512)
    tiles = c // ct

    def body(pos, mine_ref, passed_ref, dep_ref, *rest):
        o_ref = rest[-1]
        for s, ref in enumerate((mine_ref, passed_ref)):
            @pl.when(pl.program_id(0) == s)
            def _():
                o_ref[0] = ref[...]

    def to(p, j, pos):
        core = jnp.where(p == 0, pos[0], 1 - pos[0])
        return n, 2 * core + (1 - pos[1] if other_chip else pos[1]), c0 // ct + j

    extra = () if out is None else (out,)
    return pl.pallas_call(
        body,
        out_shape=jax.ShapeDtypeStruct(shape, jnp.bfloat16),
        grid_spec=pltpu.PrefetchScalarGridSpec(
            num_scalar_prefetch=1,
            grid=(2, tiles),
            in_specs=[
                pl.BlockSpec((quarter, ct), lambda p, j, pos: (0, jnp.where(p == 0, j, tiles - 1))),
                pl.BlockSpec((quarter, ct), lambda p, j, pos: (0, jnp.where(p == 1, j, 0))),
            ]
            + [ANY] * (1 + len(extra)),
            out_specs=pl.BlockSpec((1, quarter, ct), to),
        ),
        input_output_aliases={4: 0} if extra else {},
        compiler_params=pltpu.CompilerParams(vmem_limit_bytes=VMEM),
        cost_estimate=pl.CostEstimate(flops=quarter * c * 400, bytes_accessed=quarter * c * 8, transcendentals=0),
    )(pos, mine, passed, dep, *extra)


def solution(mesh):
    over_x = [(0, 2), (2, 0), (1, 3), (3, 1)]
    over_core = [(0, 1), (1, 0), (2, 3), (3, 2)]

    def swap(t, pairs):
        return lax.ppermute(t, "dp", pairs)

    def body(a, g):
        me = lax.axis_index("dp")
        pos = jnp.stack([lax.rem(me, 2), lax.div(me, 2)]).astype(jnp.int32)
        _, matrices, _, d = a.shape
        shape = (matrices, d, g.shape[3])
        *f, z0 = reduce_to_quarters(a, g)
        z = [z0] + [swap(t, over_x) for i, t in enumerate(f) if i > 0]
        cf = [swap(t, over_core) for t in f]
        out = None
        for i, piece in enumerate(PIECES):
            out = place(pos, f[i], cf[i], out, pos, shape, *piece, False)
        for i, piece in enumerate(PIECES):
            cz = swap(z[i], over_core)
            out = place(pos, z[i], cz, out, pos, shape, *piece, True)
        return out

    spec = P(("rep", "dp"))
    return jax.shard_map(body, mesh=mesh, in_specs=(spec, spec), out_specs=P("rep"), check_vma=False)
```

time: 605 us -> 595 us (0.983)
  waiting for transfers between devices: 246 us -> 228 us
  Pallas kernels: 344 us -> 354 us
    ppermute x21 -> x23, waiting for transfers between devices: 246 us -> 228 us  [swap(): return lax.ppermute(t, 'dp', pairs)]
    pallas_call x1, Pallas kernels: 249 us -> 255 us  [reduce_to_quarters(): pl.pallas_call(reduce_kernel, out_shape=tuple((jax.ShapeDtypeStruct((quar...]
    pallas_call x14 -> x16, Pallas kernels: 95.6 us -> 98.6 us  [place(): pl.pallas_call(body, out_shape=jax.ShapeDtypeStruct(shape, jnp.bfloat16),...]
  transfers between devices with their start and end apart: 21 -> 23, of which waited for: 7 -> 10; matrix products, arithmetic and copies ran while one was open for 0% -> 0% of each run, Pallas kernels for 15% -> 16%
where the time goes in v5:
time: 595 us; the launch traced here: 593 us
  Pallas kernels  354 us (59%)
  waiting for transfers between devices  228 us (38%)
  starting transfers between devices  8.68 us (1%)
    pallas_call x1, Pallas kernels, reduce_to_quarters(): pl.pallas_call(reduce_kernel, out_shape=tuple((jax.ShapeDtypeStruct((quar...  255 us
    ppermute x23, waiting for transfers between devices, swap(): return lax.ppermute(t, 'dp', pairs)  228 us
    pallas_call x16, Pallas kernels, place(): pl.pallas_call(body, out_shape=jax.ShapeDtypeStruct(shape, jnp.bfloat16),...  98.6 us
  transfers between devices with their start and end apart: 23, of which 10 were waited for; matrix products, arithmetic and copies ran while one was open for 0% of the time, Pallas kernels for 16%

profile of v5, /device:TPU:0, one launch (start us, length us, event | category | flops | bytes accessed | tf_op | source)
XLA Modules:
  0.0 593.0 jit_solution(1154389671677758858)
XLA Ops:
  0.0 255.3 %reduce.1 = (bf16[384,512]{1,0:T(8,128)(2,1)}, bf16[384,3072]{1,0:T(8,128)(2,1)}, bf16[384,3584]{1,0:T(8,128)(2,1)}, bf16[384,3584]{1,0:T(8,128)(2,1)}, bf16[384...) custom-call(bf16[1,4,4096,1536]{3,2,1,0:T(8,128)(2,1)} %a.1, ...), custom_call_target="tpu_custom_call" | custom-call | flops 180388626432 | bytes 167772160 | tf_op jit(solution)/shard_map/reduce/pallas_call | solution.py:222
  260.4 9.1 %collective-permute-done.2.mine_ref = bf16[384,512]{1,0:T(8,128)(2,1)} collective-permute-done((bf16[384,512]{1,0:T(8,128)(2,1)}, bf16[384,512]{1,0:T(8,128)(2,1)}, u32[]{:S(2)}, u32[]{:S(2)}) %collective-permute-start.2) | collective-permute-done | bytes 393248 | tf_op jit(solution)/shard_map/ppermute | solution.py:292
  269.6 8.3 %collective-permute-done.mine_ref = bf16[384,512]{1,0:T(8,128)(2,1)S(1)} collective-permute-done((bf16[384,512]{1,0:T(8,128)(2,1)}, bf16[384,512]{1,0:T(8,128)(2,1)S(1)}, u32[]{:S(2)}, u32[]{:S(2)}) %collective-permute-start) | collective-permute-done | bytes 393248 | tf_op jit(solution)/shard_map/ppermute | solution.py:292
  279.9 14.9 %collective-permute-done.4.mine_ref = bf16[384,1024]{1,0:T(8,128)(2,1)} collective-permute-done((bf16[384,1024]{1,0:T(8,128)(2,1)}, bf16[384,1024]{1,0:T(8,128)(2,1)}, u32[]{:S(2)}, u32[]{:S(2)}) %collective-permute-start.4) | collective-permute-done | bytes 786464 | tf_op jit(solution)/shard_map/ppermute | solution.py:292
  294.8 2.0 collective-permute-start.12
  296.8 141.2 %collective-permute-done.6.mine_ref = bf16[384,1536]{1,0:T(8,128)(2,1)} collective-permute-done((bf16[384,1536]{1,0:T(8,128)(2,1)}, bf16[384,1536]{1,0:T(8,128)(2,1)}, u32[]{:S(2)}, u32[]{:S(2)}) %collective-permute-start.6) | collective-permute-done | bytes 1179680 | tf_op jit(solution)/shard_map/ppermute | solution.py:292
  439.1 48.6 %collective-permute-done.12.mine_ref = bf16[384,3072]{1,0:T(8,128)(2,1)S(1)} collective-permute-done((bf16[384,3072]{1,0:T(8,128)(2,1)}, bf16[384,3072]{1,0:T(8,128)(2,1)S(1)}, u32[]{:S(2)}, u32[]{:S(2)}) %collective-permute-start.12) | collective-permute-done | bytes 2359328 | tf_op jit(solution)/shard_map/ppermute | solution.py:292
  490.4 3.5 collective-permute-done.13.passed_ref
  494.0 2.7 shard_map.28.rest_0_
  497.1 9.5 %shard_map.29.rest_0_ = bf16[4,1536,3584]{2,1,0:T(8,128)(2,1)} custom-call(s32[2]{0:T(128)} %pad_add_fusion.pos.dep_ref, bf16[384,3072]{1,0:T(8,128)(2,1)} %get-tuple-element.20.mine_ref, bf16[384,3072]{1,0:T(8,128)(2,1)} %copy-done.1, s32[2]{0:T(128)} %pad_add_fusion.pos.dep_ref, ...), custom_call_target="tpu_custom_call", output_to_operand_aliasing={{}: (4, {})} | custom-call | flops 471859200 | bytes 9437184 | tf_op jit(solution)/shard_map/pallas_call | solution.py:268
  506.6 10.7 %shard_map.30.rest_0_ = bf16[4,1536,3584]{2,1,0:T(8,128)(2,1)} custom-call(s32[2]{0:T(128)} %pad_add_fusion.pos.dep_ref, bf16[384,3584]{1,0:T(8,128)(2,1)} %get-tuple-element.19.mine_ref, bf16[384,3584]{1,0:T(8,128)(2,1)} %collective-permute-done.20.passed_ref, s32[2]{0:T(128)} %pad_add_fusion.pos.dep_ref, ...), custom_call_target="tpu_custom_call", output_to_operand_aliasing={{}: (4, {})} | custom-call | flops 550502400 | bytes 11010048 | tf_op jit(solution)/shard_map/pallas_call | solution.py:268
  517.3 10.7 %shard_map.31.rest_0_ = bf16[4,1536,3584]{2,1,0:T(8,128)(2,1)} custom-call(s32[2]{0:T(128)} %pad_add_fusion.pos.dep_ref, bf16[384,3584]{1,0:T(8,128)(2,1)} %get-tuple-element.18.mine_ref, bf16[384,3584]{1,0:T(8,128)(2,1)} %collective-permute-done.19.passed_ref, s32[2]{0:T(128)} %pad_add_fusion.pos.dep_ref, ...), custom_call_target="tpu_custom_call", output_to_operand_aliasing={{}: (4, {})} | custom-call | flops 550502400 | bytes 11010048 | tf_op jit(solution)/shard_map/pallas_call | solution.py:268
  528.0 5.7 shard_map.32.rest_0_
  533.8 4.5 shard_map.33.rest_0_
  538.3 2.7 shard_map.34.rest_0_
  541.0 2.7 shard_map.35.rest_0_
  543.7 2.7 shard_map.36.rest_0_
  546.4 9.5 %shard_map.37.rest_0_ = bf16[4,1536,3584]{2,1,0:T(8,128)(2,1)} custom-call(s32[2]{0:T(128)} %pad_add_fusion.pos.dep_ref, bf16[384,3072]{1,0:T(8,128)(2,1)} %copy-done, bf16[384,3072]{1,0:T(8,128)(2,1)} %collective-permute-done.13.passed_ref, s32[2]{0:T(128)} %pad_add_fusion.pos.dep_ref, ...), custom_call_target="tpu_custom_call", output_to_operand_aliasing={{}: (4, {})} | custom-call | flops 471859200 | bytes 9437184 | tf_op jit(solution)/shard_map/pallas_call | solution.py:268
  555.9 10.7 %shard_map.38.rest_0_ = bf16[4,1536,3584]{2,1,0:T(8,128)(2,1)} custom-call(s32[2]{0:T(128)} %pad_add_fusion.pos.dep_ref, bf16[384,3584]{1,0:T(8,128)(2,1)} %collective-permute-done.10.mine_ref, bf16[384,3584]{1,0:T(8,128)(2,1)} %collective-permute-done.11.passed_ref, s32[2]{0:T(128)} %pad_add_fusion.pos.dep_ref, ...), custom_call_target="tpu_custom_call", output_to_operand_aliasing={{}: (4, {})} | custom-call | flops 550502400 | bytes 11010048 | tf_op jit(solution)/shard_map/pallas_call | solution.py:268
  566.6 10.7 %shard_map.39.rest_0_ = bf16[4,1536,3584]{2,1,0:T(8,128)(2,1)} custom-call(s32[2]{0:T(128)} %pad_add_fusion.pos.dep_ref, bf16[384,3584]{1,0:T(8,128)(2,1)} %collective-permute-done.8.mine_ref, bf16[384,3584]{1,0:T(8,128)(2,1)} %collective-permute-done.9.passed_ref, s32[2]{0:T(128)} %pad_add_fusion.pos.dep_ref, ...), custom_call_target="tpu_custom_call", output_to_operand_aliasing={{}: (4, {})} | custom-call | flops 550502400 | bytes 11010048 | tf_op jit(solution)/shard_map/pallas_call | solution.py:268
  577.3 5.7 shard_map.40.rest_0_
  583.1 4.5 shard_map.41.rest_0_
  587.6 2.7 shard_map.42.rest_0_
  590.3 2.7 shard_map.43
  (58 shorter events, 11.4 us)
Async XLA Ops:
  255.3 2.0 collective-permute-start.22
  255.3 2.5 collective-permute-start.16
  255.8 2.5 collective-permute-start.15
  255.8 22.0 %collective-permute-start.17 = (bf16[384,1024]{1,0:T(8,128)(2,1)}, bf16[384,1024]{1,0:T(8,128)(2,1)S(1)}, u32[]{:S(2)}, u32[]{:S(2)}) collective-permute-start(bf16[384,1024]{1,0:T(8,128)(2,1)} %get-tuple-element.16.mine_ref), channel_id=1, source_target_pairs={{0,1},{1,0},{2,3},{3,2},{4,5},{5,4},{6,7},{7,6}} | collective-permute-start | bytes 2359304 | tf_op jit(solution)/shard_map/ppermute | solution.py:292
  256.3 3.7 collective-permute-start.14
  257.2 12.3 %collective-permute-start.2 = (bf16[384,512]{1,0:T(8,128)(2,1)}, bf16[384,512]{1,0:T(8,128)(2,1)}, u32[]{:S(2)}, u32[]{:S(2)}) collective-permute-start(bf16[384,512]{1,0:T(8,128)(2,1)} %get-tuple-element.15.mine_ref), channel_id=1, source_target_pairs={{0,2},{2,0},{1,3},{3,1},{4,6},{6,4},{5,7},{7,5}} | collective-permute-start | bytes 1179656 | tf_op jit(solution)/shard_map/ppermute | solution.py:292
  257.8 37.0 %collective-permute-start.18 = (bf16[384,1536]{1,0:T(8,128)(2,1)}, bf16[384,1536]{1,0:T(8,128)(2,1)S(1)}, u32[]{:S(2)}, u32[]{:S(2)}) collective-permute-start(bf16[384,1536]{1,0:T(8,128)(2,1)} %get-tuple-element.17.mine_ref), channel_id=1, source_target_pairs={{0,1},{1,0},{2,3},{3,2},{4,5},{5,4},{6,7},{7,6}} | collective-permute-start | bytes 3538952 | tf_op jit(solution)/shard_map/ppermute | solution.py:292
  258.4 19.5 %collective-permute-start = (bf16[384,512]{1,0:T(8,128)(2,1)}, bf16[384,512]{1,0:T(8,128)(2,1)S(1)}, u32[]{:S(2)}, u32[]{:S(2)}) collective-permute-start(bf16[384,512]{1,0:T(8,128)(2,1)} %get-tuple-element.14.mine_ref), channel_id=1, source_target_pairs={{0,2},{2,0},{1,3},{3,1},{4,6},{6,4},{5,7},{7,5}} | collective-permute-start | bytes 1179656 | tf_op jit(solution)/shard_map/ppermute | solution.py:292
  260.0 34.8 %collective-permute-start.4 = (bf16[384,1024]{1,0:T(8,128)(2,1)}, bf16[384,1024]{1,0:T(8,128)(2,1)}, u32[]{:S(2)}, u32[]{:S(2)}) collective-permute-start(bf16[384,1024]{1,0:T(8,128)(2,1)} %get-tuple-element.16.mine_ref), channel_id=1, source_target_pairs={{0,2},{2,0},{1,3},{3,1},{4,6},{6,4},{5,7},{7,5}} | collective-permute-start | bytes 2359304 | tf_op jit(solution)/shard_map/ppermute | solution.py:292
  269.6 168.5 %collective-permute-start.21 = (bf16[384,3072]{1,0:T(8,128)(2,1)}, bf16[384,3072]{1,0:T(8,128)(2,1)S(1)}, u32[]{:S(2)}, u32[]{:S(2)}) collective-permute-start(bf16[384,3072]{1,0:T(8,128)(2,1)} %get-tuple-element.20.mine_ref), channel_id=1, source_target_pairs={{0,1},{1,0},{2,3},{3,2},{4,5},{5,4},{6,7},{7,6}} | collective-permute-start | bytes 7077896 | tf_op jit(solution)/shard_map/ppermute | solution.py:292
  277.9 211.9 %copy-start.4 = (bf16[384,512]{1,0:T(8,128)(2,1)}, bf16[384,512]{1,0:T(8,128)(2,1)S(1)}, u32[]{:S(2)}) copy-start(bf16[384,512]{1,0:T(8,128)(2,1)S(1)} %collective-permute-done.mine_ref) | copy-start | bytes 1179652
  277.9 160.7 %collective-permute-start.10 = (bf16[384,3584]{1,0:T(8,128)(2,1)}, bf16[384,3584]{1,0:T(8,128)(2,1)}, u32[]{:S(2)}, u32[]{:S(2)}) collective-permute-start(bf16[384,3584]{1,0:T(8,128)(2,1)} %get-tuple-element.19.mine_ref), channel_id=1, source_target_pairs={{0,2},{2,0},{1,3},{3,1},{4,6},{6,4},{5,7},{7,5}} | collective-permute-start | bytes 8257544 | tf_op jit(solution)/shard_map/ppermute | solution.py:292
  277.9 160.7 %collective-permute-start.8 = (bf16[384,3584]{1,0:T(8,128)(2,1)}, bf16[384,3584]{1,0:T(8,128)(2,1)}, u32[]{:S(2)}, u32[]{:S(2)}) collective-permute-start(bf16[384,3584]{1,0:T(8,128)(2,1)} %get-tuple-element.18.mine_ref), channel_id=1, source_target_pairs={{0,2},{2,0},{1,3},{3,1},{4,6},{6,4},{5,7},{7,5}} | collective-permute-start | bytes 8257544 | tf_op jit(solution)/shard_map/ppermute | solution.py:292
  294.8 143.3 %collective-permute-start.6 = (bf16[384,1536]{1,0:T(8,128)(2,1)}, bf16[384,1536]{1,0:T(8,128)(2,1)}, u32[]{:S(2)}, u32[]{:S(2)}) collective-permute-start(bf16[384,1536]{1,0:T(8,128)(2,1)} %get-tuple-element.17.mine_ref), channel_id=1, source_target_pairs={{0,2},{2,0},{1,3},{3,1},{4,6},{6,4},{5,7},{7,5}} | collective-permute-start | bytes 3538952 | tf_op jit(solution)/shard_map/ppermute | solution.py:292
  294.8 192.9 %collective-permute-start.12 = (bf16[384,3072]{1,0:T(8,128)(2,1)}, bf16[384,3072]{1,0:T(8,128)(2,1)S(1)}, u32[]{:S(2)}, u32[]{:S(2)}) collective-permute-start(bf16[384,3072]{1,0:T(8,128)(2,1)} %get-tuple-element.20.mine_ref), channel_id=1, source_target_pairs={{0,2},{2,0},{1,3},{3,1},{4,6},{6,4},{5,7},{7,5}} | collective-permute-start | bytes 7077896 | tf_op jit(solution)/shard_map/ppermute | solution.py:292
  438.1 51.1 %collective-permute-start.20 = (bf16[384,3584]{1,0:T(8,128)(2,1)}, bf16[384,3584]{1,0:T(8,128)(2,1)}, u32[]{:S(2)}, u32[]{:S(2)}) collective-permute-start(bf16[384,3584]{1,0:T(8,128)(2,1)} %get-tuple-element.19.mine_ref), channel_id=1, source_target_pairs={{0,1},{1,0},{2,3},{3,2},{4,5},{5,4},{6,7},{7,6}} | collective-permute-start | bytes 8257544 | tf_op jit(solution)/shard_map/ppermute | solution.py:292
  438.1 51.6 %collective-permute-start.19 = (bf16[384,3584]{1,0:T(8,128)(2,1)}, bf16[384,3584]{1,0:T(8,128)(2,1)}, u32[]{:S(2)}, u32[]{:S(2)}) collective-permute-start(bf16[384,3584]{1,0:T(8,128)(2,1)} %get-tuple-element.18.mine_ref), channel_id=1, source_target_pairs={{0,1},{1,0},{2,3},{3,2},{4,5},{5,4},{6,7},{7,6}} | collective-permute-start | bytes 8257544 | tf_op jit(solution)/shard_map/ppermute | solution.py:292
  438.6 58.1 %collective-permute-start.11 = (bf16[384,3584]{1,0:T(8,128)(2,1)}, bf16[384,3584]{1,0:T(8,128)(2,1)}, u32[]{:S(2)}, u32[]{:S(2)}) collective-permute-start(bf16[384,3584]{1,0:T(8,128)(2,1)} %collective-permute-done.10.mine_ref), channel_id=1, source_target_pairs={{0,1},{1,0},{2,3},{3,2},{4,5},{5,4},{6,7},{7,6}} | collective-permute-start | bytes 8257544 | tf_op jit(solution)/shard_map/ppermute | solution.py:292
  438.6 128.0 %collective-permute-start.9 = (bf16[384,3584]{1,0:T(8,128)(2,1)}, bf16[384,3584]{1,0:T(8,128)(2,1)}, u32[]{:S(2)}, u32[]{:S(2)}) collective-permute-start(bf16[384,3584]{1,0:T(8,128)(2,1)} %collective-permute-done.8.mine_ref), channel_id=1, source_target_pairs={{0,1},{1,0},{2,3},{3,2},{4,5},{5,4},{6,7},{7,6}} | collective-permute-start | bytes 8257544 | tf_op jit(solution)/shard_map/ppermute | solution.py:292
  489.2 4.7 collective-permute-start.13
  489.2 88.1 %collective-permute-start.7 = (bf16[384,1536]{1,0:T(8,128)(2,1)}, bf16[384,1536]{1,0:T(8,128)(2,1)}, u32[]{:S(2)}, u32[]{:S(2)}) collective-permute-start(bf16[384,1536]{1,0:T(8,128)(2,1)} %collective-permute-done.6.mine_ref), channel_id=1, source_target_pairs={{0,1},{1,0},{2,3},{3,2},{4,5},{5,4},{6,7},{7,6}} | collective-permute-start | bytes 3538952 | tf_op jit(solution)/shard_map/ppermute | solution.py:292
  489.7 93.3 %collective-permute-start.5 = (bf16[384,1024]{1,0:T(8,128)(2,1)}, bf16[384,1024]{1,0:T(8,128)(2,1)}, u32[]{:S(2)}, u32[]{:S(2)}) collective-permute-start(bf16[384,1024]{1,0:T(8,128)(2,1)} %collective-permute-done.4.mine_ref), channel_id=1, source_target_pairs={{0,1},{1,0},{2,3},{3,2},{4,5},{5,4},{6,7},{7,6}} | collective-permute-start | bytes 2359304 | tf_op jit(solution)/shard_map/ppermute | solution.py:292
  493.8 93.7 %collective-permute-start.3 = (bf16[384,512]{1,0:T(8,128)(2,1)}, bf16[384,512]{1,0:T(8,128)(2,1)}, u32[]{:S(2)}, u32[]{:S(2)}) collective-permute-start(bf16[384,512]{1,0:T(8,128)(2,1)} %collective-permute-done.2.mine_ref), channel_id=1, source_target_pairs={{0,1},{1,0},{2,3},{3,2},{4,5},{5,4},{6,7},{7,6}} | collective-permute-start | bytes 1179656 | tf_op jit(solution)/shard_map/ppermute | solution.py:292
  496.7 93.6 %collective-permute-start.1 = (bf16[384,512]{1,0:T(8,128)(2,1)}, bf16[384,512]{1,0:T(8,128)(2,1)}, u32[]{:S(2)}, u32[]{:S(2)}) collective-permute-start(bf16[384,512]{1,0:T(8,128)(2,1)} %copy-done.4), channel_id=1, source_target_pairs={{0,1},{1,0},{2,3},{3,2},{4,5},{5,4},{6,7},{7,6}} | collective-permute-start | bytes 1179656 | tf_op jit(solution)/shard_map/ppermute | solution.py:292
  (8 other events, 503.6 us)

commit v6 on v5

--- a/solution.py
+++ b/solution.py
@@ -8,7 +8,8 @@
 
 CT = 512
 SENDS = 8
-PIECES = ((0, 0, 512), (0, 512, 3072), (1, 0, 3584), (2, 0, 3584), (3, 0, 1536), (3, 1536, 1024), (3, 2560, 512), (3, 3072, 512))
+PIECES = ((0, 0, 512), (0, 512, 3072), (1, 0, 3584), (2, 0, 3584), (3, 0, 1536), (3, 1536, 1024), (3, 2560, 512), (3, 3072, 256), (3, 3328, 256))
+PARTS = 3
 VMEM = 67043328
 ANY = pl.BlockSpec(memory_space=pl.ANY)
 MESH = pl.DeviceIdType.MESH
@@ -75,6 +76,8 @@
 
     def store_f(u, out, c0):
         s = lax.rem(u, 2)
+        if out.shape[1] < CT:
+            return pltpu.make_async_copy(fbuf.at[s, :, pl.ds(c0 % CT, out.shape[1])], out, f_sem.at[s])
         at = pl.multiple_of(lax.rem(u, per) * CT - c0, CT)
         return pltpu.make_async_copy(fbuf.at[s], out.at[:, pl.ds(at, CT)], f_sem.at[s])
 
@@ -106,7 +109,7 @@
         for (n, c0, c), out in zip(PIECES, outs):
             lo = n * per + c0 // CT
 
-            @pl.when((u >= lo) & (u < lo + c // CT))
+            @pl.when((u >= lo) & (u < lo + pl.cdiv(c, CT)))
             def _():
                 store_f(u, out, c0).start()
 
@@ -249,39 +252,49 @@
     )(a, g)
 
 
-def place(pos, mine, passed, out, dep, shape, n, c0, c, other_chip):
-    quarter, ct = mine.shape[0], min(c, 512)
-    tiles = c // ct
-
-    def body(pos, mine_ref, passed_ref, dep_ref, *rest):
-        o_ref = rest[-1]
+def place(mine, passed, out, shape, n, c0, c, other_chip):
+    quarter = mine.shape[0]
+    rows = quarter // PARTS
+
+    def body(mine_ref, passed_ref, *rest):
+        o_ref, buf, in_sem, out_sem = rest[-4:]
+        me = lax.axis_index("dp")
+        core, x = lax.rem(me, 2), lax.div(me, 2)
+        copies = []
         for s, ref in enumerate((mine_ref, passed_ref)):
-            @pl.when(pl.program_id(0) == s)
-            def _():
-                o_ref[0] = ref[...]
-
-    def to(p, j, pos):
-        core = jnp.where(p == 0, pos[0], 1 - pos[0])
-        return n, 2 * core + (1 - pos[1] if other_chip else pos[1]), c0 // ct + j
+            first = quarter * (2 * (1 - core if s else core) + (1 - x if other_chip else x))
+            for p in range(PARTS):
+                part = buf.at[s, pl.ds(p * rows, rows)]
+                to = o_ref.at[n, pl.ds(pl.multiple_of(first + p * rows, rows), rows), pl.ds(c0, c)]
+                copies.append(
+                    (
+                        pltpu.make_async_copy(ref.at[pl.ds(p * rows, rows)], part, in_sem.at[s, p]),
+                        pltpu.make_async_copy(part, to, out_sem.at[s, p]),
+                    )
+                )
+        for load, _ in copies:
+            load.start()
+        for load, store in copies:
+            load.wait()
+            store.start()
+        for _, store in copies:
+            store.wait()
 
     extra = () if out is None else (out,)
     return pl.pallas_call(
         body,
         out_shape=jax.ShapeDtypeStruct(shape, jnp.bfloat16),
-        grid_spec=pltpu.PrefetchScalarGridSpec(
-            num_scalar_prefetch=1,
-            grid=(2, tiles),
-            in_specs=[
-                pl.BlockSpec((quarter, ct), lambda p, j, pos: (0, jnp.where(p == 0, j, tiles - 1))),
-                pl.BlockSpec((quarter, ct), lambda p, j, pos: (0, jnp.where(p == 1, j, 0))),
-            ]
-            + [ANY] * (1 + len(extra)),
-            out_specs=pl.BlockSpec((1, quarter, ct), to),
-        ),
-        input_output_aliases={4: 0} if extra else {},
+        in_specs=[ANY] * (2 + len(extra)),
+        out_specs=ANY,
+        scratch_shapes=[
+            pltpu.VMEM((2, quarter, c), jnp.bfloat16),
+            pltpu.SemaphoreType.DMA((2, PARTS)),
+            pltpu.SemaphoreType.DMA((2, PARTS)),
+        ],
+        input_output_aliases={2: 0} if extra else {},
         compiler_params=pltpu.CompilerParams(vmem_limit_bytes=VMEM),
         cost_estimate=pl.CostEstimate(flops=quarter * c * 400, bytes_accessed=quarter * c * 8, transcendentals=0),
-    )(pos, mine, passed, dep, *extra)
+    )(mine, passed, *extra)
 
 
 def solution(mesh):
@@ -292,8 +305,6 @@
         return lax.ppermute(t, "dp", pairs)
 
     def body(a, g):
-        me = lax.axis_index("dp")
-        pos = jnp.stack([lax.rem(me, 2), lax.div(me, 2)]).astype(jnp.int32)
         _, matrices, _, d = a.shape
         shape = (matrices, d, g.shape[3])
         *f, z0 = reduce_to_quarters(a, g)
@@ -301,10 +312,10 @@
         cf = [swap(t, over_core) for t in f]
         out = None
         for i, piece in enumerate(PIECES):
-            out = place(pos, f[i], cf[i], out, pos, shape, *piece, False)
+            out = place(f[i], cf[i], out, shape, *piece, False)
         for i, piece in enumerate(PIECES):
             cz = swap(z[i], over_core)
-            out = place(pos, z[i], cz, out, pos, shape, *piece, True)
+            out = place(z[i], cz, out, shape, *piece, True)
         return out
 
     spec = P(("rep", "dp"))

time: 595 us -> 549 us (0.923)
  Pallas kernels: 354 us -> 306 us
    pallas_call x16 -> x18, Pallas kernels: 98.6 us -> 51.1 us  [place(): pl.pallas_call(body, out_shape=jax.ShapeDtypeStruct(shape, jnp.bfloat16),...]
    ppermute x23 -> x26, waiting for transfers between devices: 228 us -> 226 us  [swap(): return lax.ppermute(t, 'dp', pairs)]
  transfers between devices with their start and end apart: 23 -> 26, of which waited for: 10 -> 7; matrix products, arithmetic and copies ran while one was open for 0% -> 0% of each run, Pallas kernels for 16% -> 9%
where the time goes in v6:
time: 549 us
  Pallas kernels  306 us (56%)
  waiting for transfers between devices  226 us (41%)
  starting transfers between devices  11.5 us (2%)
    pallas_call x1, Pallas kernels, reduce_to_quarters(): pl.pallas_call(reduce_kernel, out_shape=tuple((jax.ShapeDtypeStruct((quar...  255 us
    ppermute x26, waiting for transfers between devices, swap(): return lax.ppermute(t, 'dp', pairs)  226 us
    pallas_call x18, Pallas kernels, place(): pl.pallas_call(body, out_shape=jax.ShapeDtypeStruct(shape, jnp.bfloat16),...  51.1 us
    ppermute x26, starting transfers between devices, swap(): return lax.ppermute(t, 'dp', pairs)  11.5 us
  transfers between devices with their start and end apart: 26, of which 7 were waited for; matrix products, arithmetic and copies ran while one was open for 0% of the time, Pallas kernels for 9%

profile of v6, /device:TPU:0, one launch (start us, length us, event | category | flops | bytes accessed | tf_op | source)
XLA Modules:
  0.0 548.8 jit_solution(11850688516043891071)
XLA Ops:
  0.0 255.3 %reduce.1 = (bf16[384,512]{1,0:T(8,128)(2,1)}, bf16[384,3072]{1,0:T(8,128)(2,1)}, bf16[384,3584]{1,0:T(8,128)(2,1)}, bf16[384,3584]{1,0:T(8,128)(2,1)}, bf16[384...) custom-call(bf16[1,4,4096,1536]{3,2,1,0:T(8,128)(2,1)} %a.1, ...), custom_call_target="tpu_custom_call" | custom-call | flops 180388626432 | bytes 167772160 | tf_op jit(solution)/shard_map/reduce/pallas_call | solution.py:225
  255.8 2.0 collective-permute-start
  259.1 4.7 collective-permute-done.2.mine_ref
  264.5 2.6 collective-permute-done.mine_ref
  267.4 1.7 collective-permute-start.6
  269.9 9.5 %collective-permute-done.4.mine_ref = bf16[384,512]{1,0:T(8,128)(2,1)} collective-permute-done((bf16[384,512]{1,0:T(8,128)(2,1)}, bf16[384,512]{1,0:T(8,128)(2,1)}, u32[]{:S(2)}, u32[]{:S(2)}) %collective-permute-start.4) | collective-permute-done | bytes 393248 | tf_op jit(solution)/shard_map/ppermute | solution.py:305
  281.4 14.8 %collective-permute-done.6.mine_ref = bf16[384,1024]{1,0:T(8,128)(2,1)} collective-permute-done((bf16[384,1024]{1,0:T(8,128)(2,1)}, bf16[384,1024]{1,0:T(8,128)(2,1)}, u32[]{:S(2)}, u32[]{:S(2)}) %collective-permute-start.6) | collective-permute-done | bytes 786464 | tf_op jit(solution)/shard_map/ppermute | solution.py:305
  298.3 141.2 %collective-permute-done.8.mine_ref = bf16[384,1536]{1,0:T(8,128)(2,1)} collective-permute-done((bf16[384,1536]{1,0:T(8,128)(2,1)}, bf16[384,1536]{1,0:T(8,128)(2,1)}, u32[]{:S(2)}, u32[]{:S(2)}) %collective-permute-start.8) | collective-permute-done | bytes 1179680 | tf_op jit(solution)/shard_map/ppermute | solution.py:305
  440.6 48.9 %collective-permute-done.14.mine_ref = bf16[384,3072]{1,0:T(8,128)(2,1)S(1)} collective-permute-done((bf16[384,3072]{1,0:T(8,128)(2,1)}, bf16[384,3072]{1,0:T(8,128)(2,1)S(1)}, u32[]{:S(2)}, u32[]{:S(2)}) %collective-permute-start.14) | collective-permute-done | bytes 2359328 | tf_op jit(solution)/shard_map/ppermute | solution.py:305
  491.5 4.0 collective-permute-done.15.passed_ref
  497.0 2.0 shard_map.28.rest_0_
  499.0 4.0 shard_map.29.rest_0_
  503.0 4.7 shard_map.30.rest_0_
  507.7 4.7 shard_map.31.rest_0_
  512.5 2.5 shard_map.32.rest_0_
  515.0 2.2 shard_map.33.rest_0_
  517.2 2.0 shard_map.34.rest_0_
  523.2 2.0 shard_map.37.rest_0_
  525.2 4.0 shard_map.38.rest_0_
  529.1 4.7 shard_map.39.rest_0_
  533.9 4.7 shard_map.40.rest_0_
  538.6 2.5 shard_map.41.rest_0_
  541.2 2.2 shard_map.42.rest_0_
  543.4 2.0 shard_map.43.rest_0_
  (69 shorter events, 19.7 us)
Async XLA Ops:
  255.8 8.0 %collective-permute-start.2 = (bf16[384,256]{1,0:T(8,128)(2,1)}, bf16[384,256]{1,0:T(8,128)(2,1)S(1)}, u32[]{:S(2)}, u32[]{:S(2)}) collective-permute-start(bf16[384,256]{1,0:T(8,128)(2,1)} %get-tuple-element.16.mine_ref), channel_id=1, source_target_pairs={{0,2},{2,0},{1,3},{3,1},{4,6},{6,4},{5,7},{7,5}} | collective-permute-start | bytes 589832 | tf_op jit(solution)/shard_map/ppermute | solution.py:305
  255.8 11.3 %collective-permute-start = (bf16[384,256]{1,0:T(8,128)(2,1)}, bf16[384,256]{1,0:T(8,128)(2,1)S(1)}, u32[]{:S(2)}, u32[]{:S(2)}) collective-permute-start(bf16[384,256]{1,0:T(8,128)(2,1)} %get-tuple-element.15.mine_ref), channel_id=1, source_target_pairs={{0,2},{2,0},{1,3},{3,1},{4,6},{6,4},{5,7},{7,5}} | collective-permute-start | bytes 589832 | tf_op jit(solution)/shard_map/ppermute | solution.py:305
  257.8 9.2 %collective-permute-start.25 = (bf16[384,512]{1,0:T(8,128)(2,1)}, bf16[384,512]{1,0:T(8,128)(2,1)S(1)}, u32[]{:S(2)}, u32[]{:S(2)}) collective-permute-start(bf16[384,512]{1,0:T(8,128)(2,1)} %get-tuple-element.24.mine_ref), channel_id=1, source_target_pairs={{0,1},{1,0},{2,3},{3,2},{4,5},{5,4},{6,7},{7,6}} | collective-permute-start | bytes 1179656 | tf_op jit(solution)/shard_map/ppermute | solution.py:305
  257.8 21.9 %collective-permute-start.20 = (bf16[384,1024]{1,0:T(8,128)(2,1)}, bf16[384,1024]{1,0:T(8,128)(2,1)S(1)}, u32[]{:S(2)}, u32[]{:S(2)}) collective-permute-start(bf16[384,1024]{1,0:T(8,128)(2,1)} %get-tuple-element.18.mine_ref), channel_id=1, source_target_pairs={{0,1},{1,0},{2,3},{3,2},{4,5},{5,4},{6,7},{7,6}} | collective-permute-start | bytes 2359304 | tf_op jit(solution)/shard_map/ppermute | solution.py:305
  259.0 8.4 %collective-permute-start.19 = (bf16[384,512]{1,0:T(8,128)(2,1)}, bf16[384,512]{1,0:T(8,128)(2,1)S(1)}, u32[]{:S(2)}, u32[]{:S(2)}) collective-permute-start(bf16[384,512]{1,0:T(8,128)(2,1)} %get-tuple-element.17.mine_ref), channel_id=1, source_target_pairs={{0,1},{1,0},{2,3},{3,2},{4,5},{5,4},{6,7},{7,6}} | collective-permute-start | bytes 1179656 | tf_op jit(solution)/shard_map/ppermute | solution.py:305
  264.5 4.7 collective-permute-start.16
  267.1 29.5 %collective-permute-start.21 = (bf16[384,1536]{1,0:T(8,128)(2,1)}, bf16[384,1536]{1,0:T(8,128)(2,1)}, u32[]{:S(2)}, u32[]{:S(2)}) collective-permute-start(bf16[384,1536]{1,0:T(8,128)(2,1)} %get-tuple-element.19.mine_ref), channel_id=1, source_target_pairs={{0,1},{1,0},{2,3},{3,2},{4,5},{5,4},{6,7},{7,6}} | collective-permute-start | bytes 3538952 | tf_op jit(solution)/shard_map/ppermute | solution.py:305
  267.1 12.3 %collective-permute-start.4 = (bf16[384,512]{1,0:T(8,128)(2,1)}, bf16[384,512]{1,0:T(8,128)(2,1)}, u32[]{:S(2)}, u32[]{:S(2)}) collective-permute-start(bf16[384,512]{1,0:T(8,128)(2,1)} %get-tuple-element.17.mine_ref), channel_id=1, source_target_pairs={{0,2},{2,0},{1,3},{3,1},{4,6},{6,4},{5,7},{7,5}} | collective-permute-start | bytes 1179656 | tf_op jit(solution)/shard_map/ppermute | solution.py:305
  267.4 28.9 %collective-permute-start.6 = (bf16[384,1024]{1,0:T(8,128)(2,1)}, bf16[384,1024]{1,0:T(8,128)(2,1)}, u32[]{:S(2)}, u32[]{:S(2)}) collective-permute-start(bf16[384,1024]{1,0:T(8,128)(2,1)} %get-tuple-element.18.mine_ref), channel_id=1, source_target_pairs={{0,2},{2,0},{1,3},{3,1},{4,6},{6,4},{5,7},{7,5}} | collective-permute-start | bytes 2359304 | tf_op jit(solution)/shard_map/ppermute | solution.py:305
  269.9 169.6 %collective-permute-start.24 = (bf16[384,3072]{1,0:T(8,128)(2,1)}, bf16[384,3072]{1,0:T(8,128)(2,1)S(1)}, u32[]{:S(2)}, u32[]{:S(2)}) collective-permute-start(bf16[384,3072]{1,0:T(8,128)(2,1)} %get-tuple-element.22.mine_ref), channel_id=1, source_target_pairs={{0,1},{1,0},{2,3},{3,2},{4,5},{5,4},{6,7},{7,6}} | collective-permute-start | bytes 7077896 | tf_op jit(solution)/shard_map/ppermute | solution.py:305
  279.4 160.6 %collective-permute-start.12 = (bf16[384,3584]{1,0:T(8,128)(2,1)}, bf16[384,3584]{1,0:T(8,128)(2,1)}, u32[]{:S(2)}, u32[]{:S(2)}) collective-permute-start(bf16[384,3584]{1,0:T(8,128)(2,1)} %get-tuple-element.21.mine_ref), channel_id=1, source_target_pairs={{0,2},{2,0},{1,3},{3,1},{4,6},{6,4},{5,7},{7,5}} | collective-permute-start | bytes 8257544 | tf_op jit(solution)/shard_map/ppermute | solution.py:305
  279.7 160.4 %collective-permute-start.10 = (bf16[384,3584]{1,0:T(8,128)(2,1)}, bf16[384,3584]{1,0:T(8,128)(2,1)}, u32[]{:S(2)}, u32[]{:S(2)}) collective-permute-start(bf16[384,3584]{1,0:T(8,128)(2,1)} %get-tuple-element.20.mine_ref), channel_id=1, source_target_pairs={{0,2},{2,0},{1,3},{3,1},{4,6},{6,4},{5,7},{7,5}} | collective-permute-start | bytes 8257544 | tf_op jit(solution)/shard_map/ppermute | solution.py:305
  296.3 143.3 %collective-permute-start.8 = (bf16[384,1536]{1,0:T(8,128)(2,1)}, bf16[384,1536]{1,0:T(8,128)(2,1)}, u32[]{:S(2)}, u32[]{:S(2)}) collective-permute-start(bf16[384,1536]{1,0:T(8,128)(2,1)} %get-tuple-element.19.mine_ref), channel_id=1, source_target_pairs={{0,2},{2,0},{1,3},{3,1},{4,6},{6,4},{5,7},{7,5}} | collective-permute-start | bytes 3538952 | tf_op jit(solution)/shard_map/ppermute | solution.py:305
  296.6 192.9 %collective-permute-start.14 = (bf16[384,3072]{1,0:T(8,128)(2,1)}, bf16[384,3072]{1,0:T(8,128)(2,1)S(1)}, u32[]{:S(2)}, u32[]{:S(2)}) collective-permute-start(bf16[384,3072]{1,0:T(8,128)(2,1)} %get-tuple-element.22.mine_ref), channel_id=1, source_target_pairs={{0,2},{2,0},{1,3},{3,1},{4,6},{6,4},{5,7},{7,5}} | collective-permute-start | bytes 7077896 | tf_op jit(solution)/shard_map/ppermute | solution.py:305
  439.5 51.4 %collective-permute-start.23 = (bf16[384,3584]{1,0:T(8,128)(2,1)}, bf16[384,3584]{1,0:T(8,128)(2,1)}, u32[]{:S(2)}, u32[]{:S(2)}) collective-permute-start(bf16[384,3584]{1,0:T(8,128)(2,1)} %get-tuple-element.21.mine_ref), channel_id=1, source_target_pairs={{0,1},{1,0},{2,3},{3,2},{4,5},{5,4},{6,7},{7,6}} | collective-permute-start | bytes 8257544 | tf_op jit(solution)/shard_map/ppermute | solution.py:305
  439.5 51.9 %collective-permute-start.22 = (bf16[384,3584]{1,0:T(8,128)(2,1)}, bf16[384,3584]{1,0:T(8,128)(2,1)}, u32[]{:S(2)}, u32[]{:S(2)}) collective-permute-start(bf16[384,3584]{1,0:T(8,128)(2,1)} %get-tuple-element.20.mine_ref), channel_id=1, source_target_pairs={{0,1},{1,0},{2,3},{3,2},{4,5},{5,4},{6,7},{7,6}} | collective-permute-start | bytes 8257544 | tf_op jit(solution)/shard_map/ppermute | solution.py:305
  440.0 82.6 %collective-permute-start.13 = (bf16[384,3584]{1,0:T(8,128)(2,1)}, bf16[384,3584]{1,0:T(8,128)(2,1)}, u32[]{:S(2)}, u32[]{:S(2)}) collective-permute-start(bf16[384,3584]{1,0:T(8,128)(2,1)} %collective-permute-done.12.mine_ref), channel_id=1, source_target_pairs={{0,1},{1,0},{2,3},{3,2},{4,5},{5,4},{6,7},{7,6}} | collective-permute-start | bytes 8257544 | tf_op jit(solution)/shard_map/ppermute | solution.py:305
  440.1 83.0 %collective-permute-start.11 = (bf16[384,3584]{1,0:T(8,128)(2,1)}, bf16[384,3584]{1,0:T(8,128)(2,1)}, u32[]{:S(2)}, u32[]{:S(2)}) collective-permute-start(bf16[384,3584]{1,0:T(8,128)(2,1)} %collective-permute-done.10.mine_ref), channel_id=1, source_target_pairs={{0,1},{1,0},{2,3},{3,2},{4,5},{5,4},{6,7},{7,6}} | collective-permute-start | bytes 8257544 | tf_op jit(solution)/shard_map/ppermute | solution.py:305
  491.0 4.5 collective-permute-start.15
  491.0 47.7 %collective-permute-start.9 = (bf16[384,1536]{1,0:T(8,128)(2,1)}, bf16[384,1536]{1,0:T(8,128)(2,1)}, u32[]{:S(2)}, u32[]{:S(2)}) collective-permute-start(bf16[384,1536]{1,0:T(8,128)(2,1)} %collective-permute-done.8.mine_ref), channel_id=1, source_target_pairs={{0,1},{1,0},{2,3},{3,2},{4,5},{5,4},{6,7},{7,6}} | collective-permute-start | bytes 3538952 | tf_op jit(solution)/shard_map/ppermute | solution.py:305
  491.5 49.7 %collective-permute-start.7 = (bf16[384,1024]{1,0:T(8,128)(2,1)}, bf16[384,1024]{1,0:T(8,128)(2,1)}, u32[]{:S(2)}, u32[]{:S(2)}) collective-permute-start(bf16[384,1024]{1,0:T(8,128)(2,1)} %collective-permute-done.6.mine_ref), channel_id=1, source_target_pairs={{0,1},{1,0},{2,3},{3,2},{4,5},{5,4},{6,7},{7,6}} | collective-permute-start | bytes 2359304 | tf_op jit(solution)/shard_map/ppermute | solution.py:305
  496.9 46.4 %collective-permute-start.5 = (bf16[384,512]{1,0:T(8,128)(2,1)}, bf16[384,512]{1,0:T(8,128)(2,1)}, u32[]{:S(2)}, u32[]{:S(2)}) collective-permute-start(bf16[384,512]{1,0:T(8,128)(2,1)} %collective-permute-done.4.mine_ref), channel_id=1, source_target_pairs={{0,1},{1,0},{2,3},{3,2},{4,5},{5,4},{6,7},{7,6}} | collective-permute-start | bytes 1179656 | tf_op jit(solution)/shard_map/ppermute | solution.py:305
  522.7 22.7 %collective-permute-start.3 = (bf16[384,256]{1,0:T(8,128)(2,1)}, bf16[384,256]{1,0:T(8,128)(2,1)}, u32[]{:S(2)}, u32[]{:S(2)}) collective-permute-start(bf16[384,256]{1,0:T(8,128)(2,1)} %copy-done.8), channel_id=1, source_target_pairs={{0,1},{1,0},{2,3},{3,2},{4,5},{5,4},{6,7},{7,6}} | collective-permute-start | bytes 589832 | tf_op jit(solution)/shard_map/ppermute | solution.py:305
  523.1 24.0 %collective-permute-start.1 = (bf16[384,256]{1,0:T(8,128)(2,1)}, bf16[384,256]{1,0:T(8,128)(2,1)}, u32[]{:S(2)}, u32[]{:S(2)}) collective-permute-start(bf16[384,256]{1,0:T(8,128)(2,1)} %copy-done.7), channel_id=1, source_target_pairs={{0,1},{1,0},{2,3},{3,2},{4,5},{5,4},{6,7},{7,6}} | collective-permute-start | bytes 589832 | tf_op jit(solution)/shard_map/ppermute | solution.py:305
  (13 other events, 95.3 us)
